TPU v7x, 256 devices: a whole 4x4x8 slice. The times are simulated.
256 devices in a mesh: pp: 4 (over x), cp: 64 (over z, y, core).
Axes of the slice: x: 4, y: 4, z: 8, core: 2. Of those that a mesh axis runs over, the one named last changes fastest.
Arguments:
- x_in: bfloat16 [4, 8192, 2048], P(None, 'cp'), may hold values from -60 to 80
- norm_gain: float32 [4, 2048], P('pp'), may hold values from 0.5 to 1.5
- w_qkv: bfloat16 [4, 2048, 3072], P('pp', 'cp'), may hold values from -0.13258252 to 1.307771
- w_out: bfloat16 [4, 2048, 2048], P('pp', 'cp'), may hold values from -0.125 to 0.125
- cycle_size: int32 [4], replicated, may hold values from 2 to 8, as said below
- token_pos: int32 [4, 8192], replicated, may hold values from 0 to 8191, as said below
- doc_starts: int32 [4, 128], replicated, may hold values from 0 to 8192, as said below
Outputs:
- layer_outputs: bfloat16 [4, 4, 8192, 2048], P('pp', None, 'cp')
Inputs may be any that keep to these rules, and one draw needn't show every extreme that they name: `cycle_size`: powers of two dividing the devices of cp; some micro-batch has 8 and some has 2. `token_pos`: for a micro-batch with group size r, every aligned block of r * 128 slots holds each position of that block once. `doc_starts`: for a micro-batch with group size r and g below 64 / r, entry 2 g is g * r * 128 and entry 2 g + 1 either lies strictly inside that group's positions or is 8192, so each group holds one or two documents; the remaining entries are 8192.
All inputs are finite; a program needn't handle non-finite values.
Results may differ from a plain program's by a relative error of at most 0.0075.
Values may be sent and summed in bfloat16 or wider, within the bound.
A program may use at most 128 MiB of HBM per device.

v0:
```python
import jax
import jax.numpy as jnp
from jax import lax
from jax.sharding import PartitionSpec as P

HEADS = 16
KV_HEADS = 4
HEAD_DIM = 128
CYCLE_MAX = 8


epsilon = 1e-05
rope_base = 500000.0


def swapped(array, axis, stride):
    return lax.ppermute(array, axis, [(i, i ^ 1 << stride) for i in range(lax.axis_size(axis))])


def side_by_side(arrays, axis, dim, along):
    both = jnp.concatenate(arrays, axis=along)
    out, at, finished = (lax.all_gather(both, axis, axis=dim, tiled=True), 0, [])
    for a in arrays:
        finished.append(lax.slice_in_dim(out, at, at + a.shape[along], axis=along))
        at += a.shape[along]
    return tuple(finished)


def from_behind(value, axis, steps):
    count = lax.axis_size(axis)
    leading, last = (max(0, -steps), min(count, count - steps))
    return lax.ppermute(value, axis, [(source, source + steps) for source in range(leading, last)])


def rotate(values, relative):
    half_dim = values.shape[-1] // 2
    frequency_index = jnp.arange(half_dim, dtype=jnp.float32)
    inverse = jnp.power(jnp.float32(rope_base), -2.0 * frequency_index / values.shape[-1])
    angles = relative.astype(jnp.float32)[:, None] * inverse[None, :]
    cosine = jnp.cos(angles)[:, None, :]
    sine_part = jnp.sin(angles)[:, None, :]
    first_half = values[..., :half_dim]
    second_half = values[..., half_dim:]
    return jnp.concatenate(
        [
            first_half * cosine - second_half * sine_part,
            second_half * cosine + first_half * sine_part,
        ],
        axis=-1,
    )


def doc_begin(positions, starts):
    at_or_below = starts[None, :] <= positions[:, None]
    return jnp.max(jnp.where(at_or_below, starts[None, :], 0), axis=1)


def collect_keys(own_piece, device):
    tok_rows, piece_cols = own_piece.shape
    bit_total = CYCLE_MAX.bit_length() - 1
    bit_order = list(reversed(range(bit_total)))
    key_block = own_piece[None]
    for bit_index in bit_order:
        partner = swapped(key_block, "cp", bit_index)
        upper_half = device // (1 << bit_index) % 2 == 1
        key_block = jnp.where(
            upper_half,
            jnp.concatenate([partner, key_block], axis=0),
            jnp.concatenate([key_block, partner], axis=0),
        )
    shaped = key_block.reshape((2,) * bit_total + (tok_rows, piece_cols))
    flipped = tuple(reversed(range(bit_total))) + (bit_total, bit_total + 1)
    key_block = jnp.transpose(shaped, flipped)
    return key_block.reshape(CYCLE_MAX * tok_rows, piece_cols)


def attend_block(queries, key_block, query_pos, key_pos, starts, cycle_devices):
    tok_rows = queries.shape[0]
    key_cols = KV_HEADS * HEAD_DIM
    grouped = queries.reshape(tok_rows, KV_HEADS, HEADS // KV_HEADS, HEAD_DIM)
    key_part = key_block[:, :key_cols].reshape(-1, KV_HEADS, HEAD_DIM)
    value_part = key_block[:, key_cols:].reshape(-1, KV_HEADS, HEAD_DIM)
    scores = jnp.einsum(
        "bkgd,skd->kgbs", grouped, key_part, preferred_element_type=jnp.float32
    ) * HEAD_DIM ** (-0.5)
    span = cycle_devices * tok_rows
    query_begin = doc_begin(query_pos, starts)
    key_begin = doc_begin(key_pos, starts)
    visible = (
        ((query_pos // span)[:, None] == (key_pos // span)[None, :])
        & (query_begin[:, None] == key_begin[None, :])
        & (key_pos[None, :] <= query_pos[:, None])
    )
    scores = jnp.where(visible[None, None], scores, -1e30)
    row_max = jnp.max(scores, axis=-1, keepdims=True)
    weights_exp = jnp.exp(scores - row_max)
    row_sum = jnp.sum(weights_exp, axis=-1, keepdims=True)
    combined = (
        jnp.einsum(
            "kgbs,skd->kgbd",
            weights_exp.astype(jnp.bfloat16),
            value_part,
            preferred_element_type=jnp.float32,
        )
        / row_sum
    )
    return (
        jnp.transpose(combined, (2, 0, 1, 3))
        .reshape(tok_rows, HEADS * HEAD_DIM)
        .astype(jnp.bfloat16)
    )


def body(x_in, norm_gain, w_qkv, w_out, cycle_size, token_pos, doc_starts):
    sections = lax.axis_size("pp")
    section_index = lax.axis_index("pp")
    device = lax.axis_index("cp")
    micro_count, tok_rows, model_width = x_in.shape
    query_cols = HEADS * HEAD_DIM
    key_cols = KV_HEADS * HEAD_DIM
    gain_row = norm_gain[0]
    out_full = None
    qkv_gathered, out_gathered = side_by_side((w_qkv, w_out), "cp", 1, 2)
    qkv_full = qkv_gathered[0]
    out_full = out_gathered[0]
    carried = jnp.zeros((tok_rows, model_width), jnp.bfloat16)
    outputs = jnp.zeros((micro_count, tok_rows, model_width), jnp.bfloat16)
    turn_count = micro_count + sections - 1
    for turn_index in range(turn_count):
        offset = turn_index - section_index
        active = (offset >= 0) & (offset < micro_count)
        micro_index = jnp.clip(offset, 0, micro_count - 1)
        fresh_input = lax.dynamic_index_in_dim(x_in, micro_index, 0, keepdims=False)
        hidden = jnp.where(section_index == 0, fresh_input, carried)
        positions = lax.dynamic_index_in_dim(token_pos, micro_index, 0, keepdims=False)
        starts = lax.dynamic_index_in_dim(doc_starts, micro_index, 0, keepdims=False)
        cycle_devices = lax.dynamic_index_in_dim(cycle_size, micro_index, 0, keepdims=False)
        own_pos = lax.dynamic_slice_in_dim(positions, device * tok_rows, tok_rows)

        def front_work(layer_input):
            widened = layer_input.astype(jnp.float32)
            mean_square = jnp.mean(widened * widened, axis=-1, keepdims=True)
            normed = (widened * lax.rsqrt(mean_square + epsilon) * gain_row).astype(jnp.bfloat16)
            projected = jnp.dot(normed, qkv_full, preferred_element_type=jnp.float32)
            relative = own_pos - doc_begin(own_pos, starts)
            queries = rotate(
                projected[:, :query_cols].reshape(tok_rows, HEADS, HEAD_DIM), relative
            ).astype(jnp.bfloat16)
            keys_own = rotate(
                projected[:, query_cols : query_cols + key_cols].reshape(
                    tok_rows, KV_HEADS, HEAD_DIM
                ),
                relative,
            ).astype(jnp.bfloat16)
            values_own = projected[:, query_cols + key_cols :].astype(jnp.bfloat16)
            return (
                queries,
                jnp.concatenate([keys_own.reshape(tok_rows, key_cols), values_own], axis=1),
            )

        def front_empty(layer_input):
            return (
                jnp.zeros((tok_rows, HEADS, HEAD_DIM), jnp.bfloat16),
                jnp.zeros((tok_rows, 2 * key_cols), jnp.bfloat16),
            )

        queries, own_piece = lax.cond(active, front_work, front_empty, hidden)
        key_block = collect_keys(own_piece, device)
        block_start = device // CYCLE_MAX * CYCLE_MAX
        key_pos = lax.dynamic_slice_in_dim(positions, block_start * tok_rows, CYCLE_MAX * tok_rows)
        out_matrix = out_full

        def back_work(layer_input):
            attended = attend_block(queries, key_block, own_pos, key_pos, starts, cycle_devices)
            return (
                layer_input.astype(jnp.float32)
                + jnp.dot(attended, out_matrix, preferred_element_type=jnp.float32)
            ).astype(jnp.bfloat16)

        def back_empty(layer_input):
            return jnp.zeros((tok_rows, model_width), jnp.bfloat16)

        result = lax.cond(active, back_work, back_empty, hidden)
        outputs = jnp.where(
            active, lax.dynamic_update_index_in_dim(outputs, result, micro_index, 0), outputs
        )
        if turn_index + 1 < turn_count:
            carried = from_behind(result, "pp", 1)
    return outputs[None]


def solution(mesh):
    in_specs = (
        P(None, "cp", None),
        P("pp", None),
        P("pp", "cp", None),
        P("pp", "cp", None),
        P(),
        P(),
        P(),
    )
    out_specs = P("pp", None, "cp", None)
    return jax.shard_map(body, mesh=mesh, in_specs=in_specs, out_specs=out_specs, check_vma=False)
```

profile of v0, /device:TPU:7, one launch (start us, length us, event | category | flops | bytes accessed | tf_op | source)
XLA Modules:
  0.0 675.2 jit_solution(16054701769929100023)
XLA Ops:
  11.2 112.2 %all-gather.2.cloned.1.call-done = bf16[1,2048,5120]{2,1,0:T(8,128)(2,1)} async-done(((bf16[1,32,5120]{2,1,0:T(8,128)(2,1)}), bf16[1,2048,5120]{2,1,0:T(8,128)(2,1)}) %all-gather.2.cloned.1.call-update) | async-done | bytes 20971536 | tf_op jit(solution)/shard_map/all_gather | solution.py:22
  123.4 6.2 slice_bitcast_fusion.7
  129.7 4.4 copy-done
  135.5 7.9 %collective-permute-done = bf16[1,128,1024]{2,1,0:T(8,128)(2,1)S(1)} collective-permute-done((bf16[1,128,1024]{2,1,0:T(8,128)(2,1)S(1)}, bf16[1,128,1024]{2,1,0:T(8,128)(2,1)S(1)}, u32[]{:S(2)}, u32[]{:S(2)}) %collective-permute-start) | collective-permute-done | bytes 262176 | tf_op jit(solution)/shard_map/ppermute | solution.py:17
  143.7 12.3 %collective-permute-done.1 = bf16[2,128,1024]{2,1,0:T(8,128)(2,1)S(1)} collective-permute-done((bf16[2,128,1024]{2,1,0:T(8,128)(2,1)S(1)}, bf16[2,128,1024]{2,1,0:T(8,128)(2,1)S(1)}, u32[]{:S(2)}, u32[]{:S(2)}) %collective-permute-start.1) | collective-permute-done | bytes 524320 | tf_op jit(solution)/shard_map/ppermute | solution.py:17
  158.2 8.3 %slice_bitcast_fusion.8 = bf16[2048,2048]{1,0:T(8,128)(2,1)} fusion(bf16[1,2048,5120]{2,1,0:T(8,128)(2,1)} %all-gather.2.cloned.1.call-done), kind=kLoop, calls=%fused_computation.317 | loop fusion | bytes 16777216 | tf_op jit(solution)/shard_map/squeeze | solution.py:125
  168.1 4.7 copy.70
  176.2 14.3 %collective-permute-done.3 = bf16[128,2048]{1,0:T(8,128)(2,1)S(1)} collective-permute-done((bf16[128,2048]{1,0:T(8,128)(2,1)}, bf16[128,2048]{1,0:T(8,128)(2,1)S(1)}, u32[]{:S(2)}, u32[]{:S(2)}) %collective-permute-start.3) | collective-permute-done | bytes 524320 | tf_op jit(solution)/shard_map/ppermute | solution.py:32
  193.2 7.3 %collective-permute-done.4 = bf16[1,128,1024]{2,1,0:T(8,128)(2,1)S(1)} collective-permute-done((bf16[1,128,1024]{2,1,0:T(8,128)(2,1)S(1)}, bf16[1,128,1024]{2,1,0:T(8,128)(2,1)S(1)}, u32[]{:S(2)}, u32[]{:S(2)}) %collective-permute-start.4) | collective-permute-done | bytes 262176 | tf_op jit(solution)/shard_map/ppermute | solution.py:17
  200.7 11.7 %collective-permute-done.5 = bf16[2,128,1024]{2,1,0:T(8,128)(2,1)S(1)} collective-permute-done((bf16[2,128,1024]{2,1,0:T(8,128)(2,1)S(1)}, bf16[2,128,1024]{2,1,0:T(8,128)(2,1)S(1)}, u32[]{:S(2)}, u32[]{:S(2)}) %collective-permute-start.5) | collective-permute-done | bytes 524320 | tf_op jit(solution)/shard_map/ppermute | solution.py:17
  219.2 4.7 copy.72
  227.5 13.9 %collective-permute-done.7 = bf16[128,2048]{1,0:T(8,128)(2,1)S(1)} collective-permute-done((bf16[128,2048]{1,0:T(8,128)(2,1)}, bf16[128,2048]{1,0:T(8,128)(2,1)S(1)}, u32[]{:S(2)}, u32[]{:S(2)}) %collective-permute-start.7) | collective-permute-done | bytes 524320 | tf_op jit(solution)/shard_map/ppermute | solution.py:32
  244.1 7.0 %collective-permute-done.8 = bf16[1,128,1024]{2,1,0:T(8,128)(2,1)S(1)} collective-permute-done((bf16[1,128,1024]{2,1,0:T(8,128)(2,1)S(1)}, bf16[1,128,1024]{2,1,0:T(8,128)(2,1)S(1)}, u32[]{:S(2)}, u32[]{:S(2)}) %collective-permute-start.8) | collective-permute-done | bytes 262176 | tf_op jit(solution)/shard_map/ppermute | solution.py:17
  251.3 11.4 %collective-permute-done.9 = bf16[2,128,1024]{2,1,0:T(8,128)(2,1)S(1)} collective-permute-done((bf16[2,128,1024]{2,1,0:T(8,128)(2,1)S(1)}, bf16[2,128,1024]{2,1,0:T(8,128)(2,1)S(1)}, u32[]{:S(2)}, u32[]{:S(2)}) %collective-permute-start.9) | collective-permute-done | bytes 524320 | tf_op jit(solution)/shard_map/ppermute | solution.py:17
  262.8 3.0 collective-permute-start.10
  269.8 4.7 copy.74
  276.5 4.8 collective-permute-start.11
  281.3 85.3 %collective-permute-done.11 = bf16[128,2048]{1,0:T(8,128)(2,1)S(1)} collective-permute-done((bf16[128,2048]{1,0:T(8,128)(2,1)}, bf16[128,2048]{1,0:T(8,128)(2,1)S(1)}, u32[]{:S(2)}, u32[]{:S(2)}) %collective-permute-start.11) | collective-permute-done | bytes 524320 | tf_op jit(solution)/shard_map/ppermute | solution.py:32
  367.7 9.1 %conditional.20 = (bf16[128,16,128]{2,1,0:T(8,128)(2,1)S(1)}, bf16[1,128,1024]{2,1,0:T(8,128)(2,1)S(1)}) conditional(s32[]{:T(128)} %convert_element_type.255, () %tuple.156, (bf16[128,2048]{1,0:T(8,128)(2,1)S(1)}, f32[1,2048]{1,0:T(1,128)S(1)}, bf16[2048,3072]{1,0:T(8,128)(2,1)}, s32[128]{0:T(128)S(1)}, s32[128]{0:T(128)S(1)}) %tuple.312), branch_computations={%region_30.31_spmd, %region_31.34_spmd} | conditional | flops 1615651200 | bytes 24983568 | solution.py:167
  368.1 6.5 fusion.69
  378.1 7.2 %collective-permute-done.12 = bf16[1,128,1024]{2,1,0:T(8,128)(2,1)S(1)} collective-permute-done((bf16[1,128,1024]{2,1,0:T(8,128)(2,1)S(1)}, bf16[1,128,1024]{2,1,0:T(8,128)(2,1)S(1)}, u32[]{:S(2)}, u32[]{:S(2)}) %collective-permute-start.12) | collective-permute-done | bytes 262176 | tf_op jit(solution)/shard_map/ppermute | solution.py:17
  385.6 11.5 %collective-permute-done.13 = bf16[2,128,1024]{2,1,0:T(8,128)(2,1)S(1)} collective-permute-done((bf16[2,128,1024]{2,1,0:T(8,128)(2,1)S(1)}, bf16[2,128,1024]{2,1,0:T(8,128)(2,1)S(1)}, u32[]{:S(2)}, u32[]{:S(2)}) %collective-permute-start.13) | collective-permute-done | bytes 524320 | tf_op jit(solution)/shard_map/ppermute | solution.py:17
  397.3 3.2 collective-permute-start.14
  404.5 4.7 copy.76
  409.2 20.1 %conditional.21 = (bf16[128,2048]{1,0:T(8,128)(2,1)}, bf16[1,128,2048]{2,1,0:T(8,128)(2,1)}) conditional(s32[]{:T(128)} %convert_element_type.255, () %tuple.155, (bf16[128,2048]{1,0:T(8,128)(2,1)S(1)}, s32[128]{0:T(128)S(1)}, s32[4]{0:T(128)S(1)}, s32[]{:T(128)}, s32[4,8192]{1,0:T(4,128)}, /*index=5*/s32[]{:T(128)}, s32[]{:T(128)}, ...), branch_computations={%region_34.35_spmd, %region_35.40_spmd} | conditional | flops 2172964864 | bytes 76628624 | solution.py:183
  430.6 13.9 %collective-permute-done.15 = bf16[128,2048]{1,0:T(8,128)(2,1)S(1)} collective-permute-done((bf16[128,2048]{1,0:T(8,128)(2,1)}, bf16[128,2048]{1,0:T(8,128)(2,1)S(1)}, u32[]{:S(2)}, u32[]{:S(2)}) %collective-permute-start.15) | collective-permute-done | bytes 524320 | tf_op jit(solution)/shard_map/ppermute | solution.py:32
  445.6 9.3 %conditional.22 = (bf16[128,16,128]{2,1,0:T(8,128)(2,1)S(1)}, bf16[1,128,1024]{2,1,0:T(8,128)(2,1)S(1)}) conditional(s32[]{:T(128)} %convert_element_type.256, () %tuple.160, (bf16[128,2048]{1,0:T(8,128)(2,1)S(1)}, f32[1,2048]{1,0:T(1,128)S(1)}, bf16[2048,3072]{1,0:T(8,128)(2,1)}, s32[128]{0:T(128)S(1)}, s32[128]{0:T(128)S(1)}) %tuple.310), branch_computations={%region_40.41_spmd, %region_41.44_spmd} | conditional | flops 1615651200 | bytes 24983568 | solution.py:167
  446.2 6.5 fusion.91
  456.2 6.9 %collective-permute-done.16 = bf16[1,128,1024]{2,1,0:T(8,128)(2,1)S(1)} collective-permute-done((bf16[1,128,1024]{2,1,0:T(8,128)(2,1)S(1)}, bf16[1,128,1024]{2,1,0:T(8,128)(2,1)S(1)}, u32[]{:S(2)}, u32[]{:S(2)}) %collective-permute-start.16) | collective-permute-done | bytes 262176 | tf_op jit(solution)/shard_map/ppermute | solution.py:17
  463.5 11.3 %collective-permute-done.17 = bf16[2,128,1024]{2,1,0:T(8,128)(2,1)S(1)} collective-permute-done((bf16[2,128,1024]{2,1,0:T(8,128)(2,1)S(1)}, bf16[2,128,1024]{2,1,0:T(8,128)(2,1)S(1)}, u32[]{:S(2)}, u32[]{:S(2)}) %collective-permute-start.17) | collective-permute-done | bytes 524320 | tf_op jit(solution)/shard_map/ppermute | solution.py:17
  481.8 4.7 copy.78
  486.6 20.4 %conditional.23 = (bf16[128,2048]{1,0:T(8,128)(2,1)}, bf16[1,128,2048]{2,1,0:T(8,128)(2,1)}) conditional(s32[]{:T(128)} %convert_element_type.256, () %tuple.159, (bf16[128,2048]{1,0:T(8,128)(2,1)S(1)}, s32[128]{0:T(128)S(1)}, s32[4]{0:T(128)S(1)}, s32[]{:T(128)}, s32[4,8192]{1,0:T(4,128)}, /*index=5*/s32[]{:T(128)}, s32[]{:T(128)}, ...), branch_computations={%region_44.45_spmd, %region_45.50_spmd} | conditional | flops 2172964864 | bytes 76628624 | solution.py:183
  508.3 13.9 %collective-permute-done.19 = bf16[128,2048]{1,0:T(8,128)(2,1)S(1)} collective-permute-done((bf16[128,2048]{1,0:T(8,128)(2,1)}, bf16[128,2048]{1,0:T(8,128)(2,1)S(1)}, u32[]{:S(2)}, u32[]{:S(2)}) %collective-permute-start.19) | collective-permute-done | bytes 524320 | tf_op jit(solution)/shard_map/ppermute | solution.py:32
  523.3 9.3 %conditional.24 = (bf16[128,16,128]{2,1,0:T(8,128)(2,1)S(1)}, bf16[1,128,1024]{2,1,0:T(8,128)(2,1)S(1)}) conditional(s32[]{:T(128)} %convert_element_type.257, () %tuple.164, (bf16[128,2048]{1,0:T(8,128)(2,1)S(1)}, f32[1,2048]{1,0:T(1,128)S(1)}, bf16[2048,3072]{1,0:T(8,128)(2,1)}, s32[128]{0:T(128)S(1)}, s32[128]{0:T(128)S(1)}) %tuple.308), branch_computations={%region_50.51_spmd, %region_51.54_spmd} | conditional | flops 1615651200 | bytes 24983568 | solution.py:167
  524.0 6.5 fusion.113
  534.0 7.0 %collective-permute-done.20 = bf16[1,128,1024]{2,1,0:T(8,128)(2,1)S(1)} collective-permute-done((bf16[1,128,1024]{2,1,0:T(8,128)(2,1)S(1)}, bf16[1,128,1024]{2,1,0:T(8,128)(2,1)S(1)}, u32[]{:S(2)}, u32[]{:S(2)}) %collective-permute-start.20) | collective-permute-done | bytes 262176 | tf_op jit(solution)/shard_map/ppermute | solution.py:17
  541.2 11.3 %collective-permute-done.21 = bf16[2,128,1024]{2,1,0:T(8,128)(2,1)S(1)} collective-permute-done((bf16[2,128,1024]{2,1,0:T(8,128)(2,1)S(1)}, bf16[2,128,1024]{2,1,0:T(8,128)(2,1)S(1)}, u32[]{:S(2)}, u32[]{:S(2)}) %collective-permute-start.21) | collective-permute-done | bytes 524320 | tf_op jit(solution)/shard_map/ppermute | solution.py:17
  559.6 4.7 copy.80
  564.4 20.5 %conditional.25 = (bf16[128,2048]{1,0:T(8,128)(2,1)}, bf16[1,128,2048]{2,1,0:T(8,128)(2,1)}) conditional(s32[]{:T(128)} %convert_element_type.257, () %tuple.163, (bf16[128,2048]{1,0:T(8,128)(2,1)S(1)}, s32[128]{0:T(128)S(1)}, s32[4]{0:T(128)S(1)}, s32[]{:T(128)}, s32[4,8192]{1,0:T(4,128)}, /*index=5*/s32[]{:T(128)}, s32[]{:T(128)}, ...), branch_computations={%region_54.55_spmd, %region_55.60_spmd} | conditional | flops 2172964864 | bytes 76628624 | solution.py:183
  586.3 13.9 %collective-permute-done.23 = bf16[128,2048]{1,0:T(8,128)(2,1)S(1)} collective-permute-done((bf16[128,2048]{1,0:T(8,128)(2,1)}, bf16[128,2048]{1,0:T(8,128)(2,1)S(1)}, u32[]{:S(2)}, u32[]{:S(2)}) %collective-permute-start.23) | collective-permute-done | bytes 524320 | tf_op jit(solution)/shard_map/ppermute | solution.py:32
  601.3 9.2 %conditional.26 = (bf16[128,16,128]{2,1,0:T(8,128)(2,1)S(1)}, bf16[1,128,1024]{2,1,0:T(8,128)(2,1)S(1)}) conditional(s32[]{:T(128)} %convert_element_type.258, () %tuple.168, (bf16[128,2048]{1,0:T(8,128)(2,1)S(1)}, f32[1,2048]{1,0:T(1,128)S(1)}, bf16[2048,3072]{1,0:T(8,128)(2,1)}, s32[128]{0:T(128)S(1)}, s32[128]{0:T(128)S(1)}) %tuple.306), branch_computations={%region_60.61_spmd, %region_61.64_spmd} | conditional | flops 1615651200 | bytes 24983568 | solution.py:167
  601.9 6.5 fusion.135
  612.1 6.6 collective-permute-done.24
  619.3 10.9 %collective-permute-done.25 = bf16[2,128,1024]{2,1,0:T(8,128)(2,1)S(1)} collective-permute-done((bf16[2,128,1024]{2,1,0:T(8,128)(2,1)S(1)}, bf16[2,128,1024]{2,1,0:T(8,128)(2,1)S(1)}, u32[]{:S(2)}, u32[]{:S(2)}) %collective-permute-start.25) | collective-permute-done | bytes 524320 | tf_op jit(solution)/shard_map/ppermute | solution.py:17
  630.4 3.0 collective-permute-start.26
  640.1 26.0 %conditional.27 = (bf16[1,128,2048]{2,1,0:T(8,128)(2,1)}) conditional(s32[]{:T(128)} %convert_element_type.258, () %tuple.167, (bf16[128,2048]{1,0:T(8,128)(2,1)S(1)}, s32[128]{0:T(128)S(1)}, s32[4]{0:T(128)S(1)}, s32[]{:T(128)}, s32[4,8192]{1,0:T(4,128)}, /*index=5*/s32[]{:T(128)}, s32[]{:T(128)}, s32[128]{0:T(128)S(1)}, ...), branch_computations={%region_64.65_spmd, %region_65.70_spmd} | conditional | flops 2172964864 | bytes 77677160 | solution.py:183
  645.0 6.2 copy.82
  651.2 4.5 reshape.1275
  (300 shorter events, 165.5 us)
Async XLA Ops:
  6.5 116.8 %all-gather.2.cloned.1.call-start = ((), (), s32[]{:S(2)}) async-start(), calls=%async_computation | async-start | bytes 21299200 | tf_op jit(solution)/shard_map/all_gather | solution.py:22
  10.0 119.6 %copy-start.15 = (s32[128]{0:T(128)}, s32[128]{0:T(128)S(1)}, u32[]{:S(2)}) copy-start(s32[128]{0:T(128)S(1)} %get-tuple-element.766) | copy-start | bytes 1540
  10.0 119.6 %copy-start.28 = (s32[128]{0:T(128)}, s32[128]{0:T(128)S(1)}, u32[]{:S(2)}) copy-start(s32[128]{0:T(128)S(1)} %get-tuple-element.764) | copy-start | bytes 1540
  11.1 118.5 %copy-start.1 = (f32[1,2048]{1,0:T(1,128)S(1)}, f32[1,2048]{1,0:T(1,128)}, u32[]{:S(2)}) copy-start(f32[1,2048]{1,0:T(1,128)} %param.36) | copy-start | bytes 24580
  134.2 9.2 %collective-permute-start = (bf16[1,128,1024]{2,1,0:T(8,128)(2,1)S(1)}, bf16[1,128,1024]{2,1,0:T(8,128)(2,1)S(1)}, u32[]{:S(2)}, u32[]{:S(2)}) collective-permute-start(bf16[1,128,1024]{2,1,0:T(8,128)(2,1)S(1)} %get-tuple-element.425), channel_id=1, source_target_pairs={{0,4},{1,5},{2,6},{3,7},{4,0},{5,1},{6,2},{7,3},{8,12},{9,13},{10,... | collective-permute-start | bytes 786440 | tf_op jit(solution)/shard_map/ppermute | solution.py:17
  143.5 12.5 %collective-permute-start.1 = (bf16[2,128,1024]{2,1,0:T(8,128)(2,1)S(1)}, bf16[2,128,1024]{2,1,0:T(8,128)(2,1)S(1)}, u32[]{:S(2)}, u32[]{:S(2)}) collective-permute-start(bf16[2,128,1024]{2,1,0:T(8,128)(2,1)S(1)} %maximum_select_fusion.14), channel_id=1, source_target_pairs={{0,2},{1,3},{2,0},{3,1},{4,6},{5,7},{6,4},{7,5},{8,10},{9,11},{10,... | collective-permute-start | bytes 1572872 | tf_op jit(solution)/shard_map/ppermute | solution.py:17
  156.1 10.4 %collective-permute-start.2 = (bf16[4,128,1024]{2,1,0:T(8,128)(2,1)S(1)}, bf16[4,128,1024]{2,1,0:T(8,128)(2,1)S(1)}, u32[]{:S(2)}, u32[]{:S(2)}) collective-permute-start(bf16[4,128,1024]{2,1,0:T(8,128)(2,1)S(1)} %maximum_select_fusion.7), channel_id=1, source_target_pairs={{0,1},{1,0},{2,3},{3,2},{4,5},{5,4},{6,7},{7,6},{8,9},{9,8},{10,11... | collective-permute-start | bytes 3145736 | tf_op jit(solution)/shard_map/ppermute | solution.py:17
  174.8 15.6 %collective-permute-start.3 = (bf16[128,2048]{1,0:T(8,128)(2,1)}, bf16[128,2048]{1,0:T(8,128)(2,1)S(1)}, u32[]{:S(2)}, u32[]{:S(2)}) collective-permute-start(bf16[128,2048]{1,0:T(8,128)(2,1)} %get-tuple-element.428), channel_id=1, source_target_pairs={{0,64},{64,128},{128,192},{1,65},{65,129},{129,193},{2,66},{66,130... | collective-permute-start | bytes 1572872 | tf_op jit(solution)/shard_map/ppermute | solution.py:32
  191.9 32.1 %copy-start.14 = (s32[128]{0:T(128)S(1)}, s32[128]{0:T(128)}, u32[]{:S(2)}) copy-start(s32[128]{0:T(128)} %get-tuple-element.767) | copy-start | bytes 1540
  191.9 32.1 %copy-start.27 = (s32[128]{0:T(128)S(1)}, s32[128]{0:T(128)}, u32[]{:S(2)}) copy-start(s32[128]{0:T(128)} %get-tuple-element.763) | copy-start | bytes 1540
  191.9 32.1 %copy-start.31 = (s32[4]{0:T(128)S(1)}, s32[4]{0:T(128)}, u32[]{:S(2)}) copy-start(s32[4]{0:T(128)} %param.39) | copy-start | bytes 52
  191.9 8.6 %collective-permute-start.4 = (bf16[1,128,1024]{2,1,0:T(8,128)(2,1)S(1)}, bf16[1,128,1024]{2,1,0:T(8,128)(2,1)S(1)}, u32[]{:S(2)}, u32[]{:S(2)}) collective-permute-start(bf16[1,128,1024]{2,1,0:T(8,128)(2,1)S(1)} %get-tuple-element.429), channel_id=1, source_target_pairs={{0,4},{1,5},{2,6},{3,7},{4,0},{5,1},{6,2},{7,3},{8,12},{9,13},{10,... | collective-permute-start | bytes 786440 | tf_op jit(solution)/shard_map/ppermute | solution.py:17
  200.6 11.8 %collective-permute-start.5 = (bf16[2,128,1024]{2,1,0:T(8,128)(2,1)S(1)}, bf16[2,128,1024]{2,1,0:T(8,128)(2,1)S(1)}, u32[]{:S(2)}, u32[]{:S(2)}) collective-permute-start(bf16[2,128,1024]{2,1,0:T(8,128)(2,1)S(1)} %maximum_select_fusion.15), channel_id=1, source_target_pairs={{0,2},{1,3},{2,0},{3,1},{4,6},{5,7},{6,4},{7,5},{8,10},{9,11},{10,... | collective-permute-start | bytes 1572872 | tf_op jit(solution)/shard_map/ppermute | solution.py:17
  212.6 5.0 collective-permute-start.6
  226.2 15.2 %collective-permute-start.7 = (bf16[128,2048]{1,0:T(8,128)(2,1)}, bf16[128,2048]{1,0:T(8,128)(2,1)S(1)}, u32[]{:S(2)}, u32[]{:S(2)}) collective-permute-start(bf16[128,2048]{1,0:T(8,128)(2,1)} %get-tuple-element.432), channel_id=1, source_target_pairs={{0,64},{64,128},{128,192},{1,65},{65,129},{129,193},{2,66},{66,130... | collective-permute-start | bytes 1572872 | tf_op jit(solution)/shard_map/ppermute | solution.py:32
  242.8 31.7 %copy-start.12 = (s32[128]{0:T(128)S(1)}, s32[128]{0:T(128)}, u32[]{:S(2)}) copy-start(s32[128]{0:T(128)} %get-tuple-element.768) | copy-start | bytes 1540
  242.9 31.7 %copy-start.25 = (s32[128]{0:T(128)S(1)}, s32[128]{0:T(128)}, u32[]{:S(2)}) copy-start(s32[128]{0:T(128)} %get-tuple-element.762) | copy-start | bytes 1540
  242.9 31.7 %copy-start.32 = (s32[4]{0:T(128)S(1)}, s32[4]{0:T(128)}, u32[]{:S(2)}) copy-start(s32[4]{0:T(128)} %param.39) | copy-start | bytes 52
  242.9 8.2 %collective-permute-start.8 = (bf16[1,128,1024]{2,1,0:T(8,128)(2,1)S(1)}, bf16[1,128,1024]{2,1,0:T(8,128)(2,1)S(1)}, u32[]{:S(2)}, u32[]{:S(2)}) collective-permute-start(bf16[1,128,1024]{2,1,0:T(8,128)(2,1)S(1)} %get-tuple-element.433), channel_id=1, source_target_pairs={{0,4},{1,5},{2,6},{3,7},{4,0},{5,1},{6,2},{7,3},{8,12},{9,13},{10,... | collective-permute-start | bytes 786440 | tf_op jit(solution)/shard_map/ppermute | solution.py:17
  251.2 11.5 %collective-permute-start.9 = (bf16[2,128,1024]{2,1,0:T(8,128)(2,1)S(1)}, bf16[2,128,1024]{2,1,0:T(8,128)(2,1)S(1)}, u32[]{:S(2)}, u32[]{:S(2)}) collective-permute-start(bf16[2,128,1024]{2,1,0:T(8,128)(2,1)S(1)} %maximum_select_fusion.16), channel_id=1, source_target_pairs={{0,2},{1,3},{2,0},{3,1},{4,6},{5,7},{6,4},{7,5},{8,10},{9,11},{10,... | collective-permute-start | bytes 1572872 | tf_op jit(solution)/shard_map/ppermute | solution.py:17
  262.8 5.3 collective-permute-start.10
  274.6 93.1 %copy-start.22 = (s32[128]{0:T(128)S(1)}, s32[128]{0:T(128)}, u32[]{:S(2)}) copy-start(s32[128]{0:T(128)} %get-tuple-element.761) | copy-start | bytes 1540
  276.5 90.1 %collective-permute-start.11 = (bf16[128,2048]{1,0:T(8,128)(2,1)}, bf16[128,2048]{1,0:T(8,128)(2,1)S(1)}, u32[]{:S(2)}, u32[]{:S(2)}) collective-permute-start(bf16[128,2048]{1,0:T(8,128)(2,1)} %get-tuple-element.436), channel_id=1, source_target_pairs={{0,64},{64,128},{128,192},{1,65},{65,129},{129,193},{2,66},{66,130... | collective-permute-start | bytes 1572872 | tf_op jit(solution)/shard_map/ppermute | solution.py:32
  376.8 32.4 %copy-start.23 = (s32[128]{0:T(128)S(1)}, s32[128]{0:T(128)}, u32[]{:S(2)}) copy-start(s32[128]{0:T(128)} %get-tuple-element.761) | copy-start | bytes 1540
  376.8 32.4 %copy-start.33 = (s32[4]{0:T(128)S(1)}, s32[4]{0:T(128)}, u32[]{:S(2)}) copy-start(s32[4]{0:T(128)} %param.39) | copy-start | bytes 52
  376.8 8.5 %collective-permute-start.12 = (bf16[1,128,1024]{2,1,0:T(8,128)(2,1)S(1)}, bf16[1,128,1024]{2,1,0:T(8,128)(2,1)S(1)}, u32[]{:S(2)}, u32[]{:S(2)}) collective-permute-start(bf16[1,128,1024]{2,1,0:T(8,128)(2,1)S(1)} %get-tuple-element.437), channel_id=1, source_target_pairs={{0,4},{1,5},{2,6},{3,7},{4,0},{5,1},{6,2},{7,3},{8,12},{9,13},{10,... | collective-permute-start | bytes 786440 | tf_op jit(solution)/shard_map/ppermute | solution.py:17
  385.4 11.8 %collective-permute-start.13 = (bf16[2,128,1024]{2,1,0:T(8,128)(2,1)S(1)}, bf16[2,128,1024]{2,1,0:T(8,128)(2,1)S(1)}, u32[]{:S(2)}, u32[]{:S(2)}) collective-permute-start(bf16[2,128,1024]{2,1,0:T(8,128)(2,1)S(1)} %maximum_select_fusion.17), channel_id=1, source_target_pairs={{0,2},{1,3},{2,0},{3,1},{4,6},{5,7},{6,4},{7,5},{8,10},{9,11},{10,... | collective-permute-start | bytes 1572872 | tf_op jit(solution)/shard_map/ppermute | solution.py:17
  397.3 5.5 collective-permute-start.14
  409.2 36.4 %copy-start.20 = (s32[128]{0:T(128)S(1)}, s32[128]{0:T(128)}, u32[]{:S(2)}) copy-start(s32[128]{0:T(128)} %get-tuple-element.760) | copy-start | bytes 1540
  429.3 15.2 %collective-permute-start.15 = (bf16[128,2048]{1,0:T(8,128)(2,1)}, bf16[128,2048]{1,0:T(8,128)(2,1)S(1)}, u32[]{:S(2)}, u32[]{:S(2)}) collective-permute-start(bf16[128,2048]{1,0:T(8,128)(2,1)} %get-tuple-element.440), channel_id=1, source_target_pairs={{0,64},{64,128},{128,192},{1,65},{65,129},{129,193},{2,66},{66,130... | collective-permute-start | bytes 1572872 | tf_op jit(solution)/shard_map/ppermute | solution.py:32
  454.9 31.7 %copy-start.21 = (s32[128]{0:T(128)S(1)}, s32[128]{0:T(128)}, u32[]{:S(2)}) copy-start(s32[128]{0:T(128)} %get-tuple-element.760) | copy-start | bytes 1540
  454.9 31.7 %copy-start.34 = (s32[4]{0:T(128)S(1)}, s32[4]{0:T(128)}, u32[]{:S(2)}) copy-start(s32[4]{0:T(128)} %param.39) | copy-start | bytes 52
  454.9 8.2 %collective-permute-start.16 = (bf16[1,128,1024]{2,1,0:T(8,128)(2,1)S(1)}, bf16[1,128,1024]{2,1,0:T(8,128)(2,1)S(1)}, u32[]{:S(2)}, u32[]{:S(2)}) collective-permute-start(bf16[1,128,1024]{2,1,0:T(8,128)(2,1)S(1)} %get-tuple-element.441), channel_id=1, source_target_pairs={{0,4},{1,5},{2,6},{3,7},{4,0},{5,1},{6,2},{7,3},{8,12},{9,13},{10,... | collective-permute-start | bytes 786440 | tf_op jit(solution)/shard_map/ppermute | solution.py:17
  463.2 11.5 %collective-permute-start.17 = (bf16[2,128,1024]{2,1,0:T(8,128)(2,1)S(1)}, bf16[2,128,1024]{2,1,0:T(8,128)(2,1)S(1)}, u32[]{:S(2)}, u32[]{:S(2)}) collective-permute-start(bf16[2,128,1024]{2,1,0:T(8,128)(2,1)S(1)} %maximum_select_fusion.18), channel_id=1, source_target_pairs={{0,2},{1,3},{2,0},{3,1},{4,6},{5,7},{6,4},{7,5},{8,10},{9,11},{10,... | collective-permute-start | bytes 1572872 | tf_op jit(solution)/shard_map/ppermute | solution.py:17
  474.9 5.3 collective-permute-start.18
  486.6 36.7 %copy-start.10 = (s32[128]{0:T(128)S(1)}, s32[128]{0:T(128)}, u32[]{:S(2)}) copy-start(s32[128]{0:T(128)} %get-tuple-element.771) | copy-start | bytes 1540
  486.6 36.7 %copy-start.18 = (s32[128]{0:T(128)S(1)}, s32[128]{0:T(128)}, u32[]{:S(2)}) copy-start(s32[128]{0:T(128)} %get-tuple-element.765) | copy-start | bytes 1540
  507.0 15.2 %collective-permute-start.19 = (bf16[128,2048]{1,0:T(8,128)(2,1)}, bf16[128,2048]{1,0:T(8,128)(2,1)S(1)}, u32[]{:S(2)}, u32[]{:S(2)}) collective-permute-start(bf16[128,2048]{1,0:T(8,128)(2,1)} %get-tuple-element.444), channel_id=1, source_target_pairs={{0,64},{64,128},{128,192},{1,65},{65,129},{129,193},{2,66},{66,130... | collective-permute-start | bytes 1572872 | tf_op jit(solution)/shard_map/ppermute | solution.py:32
  532.7 31.7 %copy-start.19 = (s32[128]{0:T(128)S(1)}, s32[128]{0:T(128)}, u32[]{:S(2)}) copy-start(s32[128]{0:T(128)} %get-tuple-element.765) | copy-start | bytes 1540
  532.7 8.2 %collective-permute-start.20 = (bf16[1,128,1024]{2,1,0:T(8,128)(2,1)S(1)}, bf16[1,128,1024]{2,1,0:T(8,128)(2,1)S(1)}, u32[]{:S(2)}, u32[]{:S(2)}) collective-permute-start(bf16[1,128,1024]{2,1,0:T(8,128)(2,1)S(1)} %get-tuple-element.445), channel_id=1, source_target_pairs={{0,4},{1,5},{2,6},{3,7},{4,0},{5,1},{6,2},{7,3},{8,12},{9,13},{10,... | collective-permute-start | bytes 786440 | tf_op jit(solution)/shard_map/ppermute | solution.py:17
  541.0 11.5 %collective-permute-start.21 = (bf16[2,128,1024]{2,1,0:T(8,128)(2,1)S(1)}, bf16[2,128,1024]{2,1,0:T(8,128)(2,1)S(1)}, u32[]{:S(2)}, u32[]{:S(2)}) collective-permute-start(bf16[2,128,1024]{2,1,0:T(8,128)(2,1)S(1)} %maximum_select_fusion.19), channel_id=1, source_target_pairs={{0,2},{1,3},{2,0},{3,1},{4,6},{5,7},{6,4},{7,5},{8,10},{9,11},{10,... | collective-permute-start | bytes 1572872 | tf_op jit(solution)/shard_map/ppermute | solution.py:17
  552.7 5.3 collective-permute-start.22
  564.4 36.9 %copy-start.9 = (s32[128]{0:T(128)S(1)}, s32[128]{0:T(128)}, u32[]{:S(2)}) copy-start(s32[128]{0:T(128)} %get-tuple-element.772) | copy-start | bytes 1540
  564.4 36.9 %copy-start.17 = (s32[128]{0:T(128)S(1)}, s32[128]{0:T(128)}, u32[]{:S(2)}) copy-start(s32[128]{0:T(128)} %get-tuple-element.759) | copy-start | bytes 1540
  585.0 15.2 %collective-permute-start.23 = (bf16[128,2048]{1,0:T(8,128)(2,1)}, bf16[128,2048]{1,0:T(8,128)(2,1)S(1)}, u32[]{:S(2)}, u32[]{:S(2)}) collective-permute-start(bf16[128,2048]{1,0:T(8,128)(2,1)} %get-tuple-element.448), channel_id=1, source_target_pairs={{0,64},{64,128},{128,192},{1,65},{65,129},{129,193},{2,66},{66,130... | collective-permute-start | bytes 1572872 | tf_op jit(solution)/shard_map/ppermute | solution.py:32
  610.5 8.2 %collective-permute-start.24 = (bf16[1,128,1024]{2,1,0:T(8,128)(2,1)S(1)}, bf16[1,128,1024]{2,1,0:T(8,128)(2,1)S(1)}, u32[]{:S(2)}, u32[]{:S(2)}) collective-permute-start(bf16[1,128,1024]{2,1,0:T(8,128)(2,1)S(1)} %get-tuple-element.449), channel_id=1, source_target_pairs={{0,4},{1,5},{2,6},{3,7},{4,0},{5,1},{6,2},{7,3},{8,12},{9,13},{10,... | collective-permute-start | bytes 786440 | tf_op jit(solution)/shard_map/ppermute | solution.py:17
  618.8 11.5 %collective-permute-start.25 = (bf16[2,128,1024]{2,1,0:T(8,128)(2,1)S(1)}, bf16[2,128,1024]{2,1,0:T(8,128)(2,1)S(1)}, u32[]{:S(2)}, u32[]{:S(2)}) collective-permute-start(bf16[2,128,1024]{2,1,0:T(8,128)(2,1)S(1)} %maximum_select_fusion.20), channel_id=1, source_target_pairs={{0,2},{1,3},{2,0},{3,1},{4,6},{5,7},{6,4},{7,5},{8,10},{9,11},{10,... | collective-permute-start | bytes 1572872 | tf_op jit(solution)/shard_map/ppermute | solution.py:17
  630.4 8.0 %collective-permute-start.26 = (bf16[4,128,1024]{2,1,0:T(8,128)(2,1)S(1)}, bf16[4,128,1024]{2,1,0:T(8,128)(2,1)S(1)}, u32[]{:S(2)}, u32[]{:S(2)}) collective-permute-start(bf16[4,128,1024]{2,1,0:T(8,128)(2,1)S(1)} %maximum_select_fusion.13), channel_id=1, source_target_pairs={{0,1},{1,0},{2,3},{3,2},{4,5},{5,4},{6,7},{7,6},{8,9},{9,8},{10,11... | collective-permute-start | bytes 3145736 | tf_op jit(solution)/shard_map/ppermute | solution.py:17
  (21 other events, 162.5 us)
Sparse Core Ops, SparseCore 0:
  10.1 113.2 all-gather.1
where the time goes:
time: 684 us; the launch traced here: 675 us
  waiting for transfers between devices  409 us (60%)
  local copies, waits for them, and re-layouts  105 us (15%)
  other arithmetic  50 us (7%)
  matrix products  48.8 us (7%)
  starting transfers between devices  41.3 us (6%)
  between operations  14.6 us (2%)
    ppermute x6, waiting for transfers between devices, from_behind(): lax.ppermute(value, axis, [(source, source + steps) for source in range(l...  155 us
    ppermute x21, waiting for transfers between devices, swapped(): lax.ppermute(array, axis, [(i, i ^ 1 << stride) for i in range(lax.axis_s...  142 us
    all_gather x1, waiting for transfers between devices, side_by_side(): lax.all_gather(both, axis, axis=dim, tiled=True)  112 us
    ppermute x21, starting transfers between devices, swapped(): lax.ppermute(array, axis, [(i, i ^ 1 << stride) for i in range(lax.axis_s...  30.1 us
    select_n x6, local copies, waits for them, and re-layouts, collect_keys(): jnp.where(upper_half, jnp.concatenate([partner, key_block], axis=0), jnp....  28.5 us
    dot_general x4, matrix products, front_work(): projected = jnp.dot(normed, qkv_full, preferred_element_type=jnp.float32)  26 us
  transfers between devices with their start and end apart: 28, of which 26 were waited for; matrix products, arithmetic and copies ran while one was open for 2% of the time, Pallas kernels for 0%

commit v1 on v0

v1 whole, which is shorter than its diff:
```python
import functools
import math

import jax
import jax.numpy as jnp
from jax import lax
from jax.experimental import pallas as pl
from jax.experimental.pallas import tpu as pltpu
from jax.sharding import PartitionSpec as P

MESH = pl.DeviceIdType.MESH
HEAD_DIM = 128
MICRO = 4
SECTIONS = 4
NY = 4
NZ = 8
BLK = 64
ROWS = 256
HALF = 1024
KVC = 512
EPS = 1e-05
ROPE_BASE = 500000.0
QSCALE = HEAD_DIM ** (-0.5) * math.log2(math.e)
N_GATHER = 176


class Comm:
    def __init__(self, ssem, rsem, home):
        self.ssem, self.rsem, self.home = ssem, rsem, home
        self.count = 0
        self.sent = []

    def make(self, src, dst, idx, dev):
        return pltpu.make_async_remote_copy(
            src_ref=src, dst_ref=dst, send_sem=self.ssem.at[idx], recv_sem=self.rsem.at[idx],
            device_id=dev, device_id_type=MESH)

    def send(self, ref, dev, dst=None):
        idx = self.count
        self.count += 1
        copy = self.make(ref, ref if dst is None else dst, idx, dev)
        copy.start()
        self.sent.append(copy)
        return idx

    def wait(self, ref, idx):
        self.make(ref, ref, idx, self.home).wait_recv()

    def drain(self):
        for copy in self.sent:
            copy.wait_send()
        self.sent = []


def kernel(wh_ref, x_ref, cos_ref, sin_ref, qpos_ref, qbeg_ref, kpos_ref, out_ref,
           wkv, wq, woa, wob, hid, kvb, qb, att, outb, bias,
           g_ssem, g_rsem, lsem, x_ssem, x_rsem, d_ssem, d_rsem, k_ssem, k_rsem, a_ssem, a_rsem, o_ssem, o_rsem):
    s = lax.axis_index("pp")
    cp = lax.axis_index("cp")
    c = cp % 2
    y = (cp // 2) % NY
    z = cp // (2 * NY)
    ym, yp, y2 = (y + NY - 1) % NY, (y + 1) % NY, (y + 2) % NY

    def dev(yy, zz, cc):
        return (s, (zz * NY + yy) * 2 + cc)

    sib = dev(y, z, 1 - c)
    dyp, dym = dev(yp, z, c), dev(ym, z, c)
    dzp, dzm = dev(y, (z + 1) % NZ, c), dev(y, (z + NZ - 1) % NZ, c)
    xnext, xprev = ((s + 1) % SECTIONS, cp), ((s + SECTIONS - 1) % SECTIONS, cp)

    barrier = pltpu.get_barrier_semaphore()
    for d in (sib, dyp, dym, dzp, dzm, xnext, xprev):
        pl.semaphore_signal(barrier, inc=1, device_id=d, device_id_type=MESH)
    pl.semaphore_wait(barrier, 7)

    comm = Comm(g_ssem, g_rsem, sib)
    mine = pl.ds(pl.multiple_of(c * 32, 32), 32)
    other = pl.ds(pl.multiple_of((1 - c) * 32, 32), 32)
    cols = ((wkv, 0, 512), (wq, 512, 1024), (woa, 1536, 512), (wob, 2048, 512))
    local, sibs = [], []
    for i, (w, at, n) in enumerate(cols):
        sibs.append(comm.send(wh_ref.at[1 - c, :, at:at + n], sib, dst=w.at[z, y, mine]))
        cpy = pltpu.make_async_copy(wh_ref.at[c, :, at:at + n], w.at[z, y, mine], lsem.at[i])
        cpy.start()
        local.append(cpy)

    toks = pl.ds(pl.multiple_of(c * 128, 128), 128)
    toks_o = pl.ds(pl.multiple_of((1 - c) * 128, 128), 128)

    def own_ready(i):
        w = cols[i][0]
        local[i].wait()
        comm.wait(w.at[z, y, other], sibs[i])

    def flood(wa, wb):
        lo, hi = pl.ds(0, 32), pl.ds(32, 32)
        a_p = comm.send(wa.at[z, y], dyp)
        a_m = comm.send(wa.at[z, y], dym)
        bz_p = comm.send(wb.at[z, y], dzp)
        bz_m = comm.send(wb.at[z, y], dzm)
        by = {}
        by[0] = (comm.send(wb.at[z, y], dyp), comm.send(wb.at[z, y], dym))
        az = {}
        az[0] = (comm.send(wa.at[z, y], dzp), comm.send(wa.at[z, y], dzm))
        comm.wait(wa.at[z, ym], a_p)
        f_p = comm.send(wa.at[z, ym, lo], dyp)
        az[1] = (comm.send(wa.at[z, ym], dzp), comm.send(wa.at[z, ym], dzm))
        comm.wait(wa.at[z, yp], a_m)
        f_m = comm.send(wa.at[z, yp, hi], dym)
        az[2] = (comm.send(wa.at[z, yp], dzp), comm.send(wa.at[z, yp], dzm))
        ycols = (y, ym, yp, y2)
        halves = []

        def y_arrivals(zz, key):
            i_p, i_m = by[key]
            comm.wait(wb.at[zz, ym], i_p)
            h_p = comm.send(wb.at[zz, ym, lo], dyp)
            comm.wait(wb.at[zz, yp], i_m)
            h_m = comm.send(wb.at[zz, yp, hi], dym)
            halves.append((zz, h_p, h_m))

        for d in (1, 2, 3):
            zm, zp = (z + NZ - d) % NZ, (z + d) % NZ
            part_p, part_m = (lo, hi) if d == 3 else (slice(None), slice(None))
            comm.wait(wb.at[zm, y], bz_p)
            n_p = comm.send(wb.at[zm, y, part_p], dzp)
            by[-d] = (comm.send(wb.at[zm, y], dyp), comm.send(wb.at[zm, y], dym))
            comm.wait(wb.at[zp, y], bz_m)
            n_m = comm.send(wb.at[zp, y, part_m], dzm)
            by[d] = (comm.send(wb.at[zp, y], dyp), comm.send(wb.at[zp, y], dym))
            bz_p, bz_m = n_p, n_m
            if d == 1:
                comm.wait(wa.at[z, y2, lo], f_p)
                comm.wait(wa.at[z, y2, hi], f_m)
                az[3] = (comm.send(wa.at[z, y2], dzp), comm.send(wa.at[z, y2], dzm))
            nxt = {}
            for k, yy in enumerate(ycols):
                comm.wait(wa.at[zm, yy], az[k][0])
                q_p = comm.send(wa.at[zm, yy, part_p], dzp)
                comm.wait(wa.at[zp, yy], az[k][1])
                q_m = comm.send(wa.at[zp, yy, part_m], dzm)
                nxt[k] = (q_p, q_m)
            az = nxt
            if d == 1:
                y_arrivals(z, 0)
            else:
                y_arrivals((z + NZ - d + 1) % NZ, -(d - 1))
                y_arrivals((z + d - 1) % NZ, d - 1)
        z4 = (z + 4) % NZ
        comm.wait(wb.at[z4, y, lo], bz_p)
        comm.wait(wb.at[z4, y, hi], bz_m)
        by[4] = (comm.send(wb.at[z4, y], dyp), comm.send(wb.at[z4, y], dym))
        for k, yy in enumerate(ycols):
            comm.wait(wa.at[z4, yy, lo], az[k][0])
            comm.wait(wa.at[z4, yy, hi], az[k][1])
        y_arrivals((z + NZ - 3) % NZ, -3)
        y_arrivals((z + 3) % NZ, 3)
        y_arrivals(z4, 4)
        for zz, h_p, h_m in halves:
            comm.wait(wb.at[zz, y2, lo], h_p)
            comm.wait(wb.at[zz, y2, hi], h_m)

    def rcopy(src, dst, ss, rs, d):
        return pltpu.make_async_remote_copy(src_ref=src, dst_ref=dst, send_sem=ss, recv_sem=rs,
                                            device_id=d, device_id_type=MESH)

    def x_local(m, h):
        return pltpu.make_async_copy(x_ref.at[m, :, h * HALF:(h + 1) * HALF], hid.at[m, h, toks], x_rsem.at[m, h])

    def x_sib(m, h):
        return rcopy(hid.at[m, h, toks], hid.at[m, h, toks], d_ssem.at[m, h], d_rsem.at[m, h], sib)

    def x_sib_in(m, h):
        return rcopy(hid.at[m, h, toks_o], hid.at[m, h, toks_o], d_ssem.at[m, h], d_rsem.at[m, h], sib)

    @pl.when(s == 0)
    def _():
        for m in range(MICRO):
            for h in range(2):
                x_local(m, h).start()

    own_ready(0)
    own_ready(1)

    @pl.when(s == 0)
    def _():
        for m in range(MICRO):
            for h in range(2):
                x_local(m, h).wait()
                x_sib(m, h).start()

    flood(wkv, wq)
    own_ready(2)
    own_ready(3)
    flood(woa, wob)

    @pl.when(s == 0)
    def _():
        for m in range(MICRO):
            for h in range(2):
                x_sib(m, h).wait_send()
                x_sib_in(m, h).wait_recv()

    def h_in(m):
        return rcopy(hid.at[m, c], hid.at[m, c], x_ssem.at[m], x_rsem.at[m, 0], xprev)

    def h_fwd(m):
        return rcopy(hid.at[m, c], hid.at[m, c], d_ssem.at[m, 0], d_rsem.at[m, 0], sib)

    def h_fwd_in(m):
        return rcopy(hid.at[m, 1 - c], hid.at[m, 1 - c], d_ssem.at[m, 0], d_rsem.at[m, 0], sib)

    def kv_out(m, i):
        return rcopy(kvb.at[m, y], kvb.at[m, y], k_ssem.at[m, i], k_rsem.at[m, i], (dyp, dym)[i])

    def kv_in(m, i):
        ref = kvb.at[m, (ym, yp)[i]]
        return rcopy(ref, ref, k_ssem.at[m, i], k_rsem.at[m, i], sib)

    def kv_half(m, i):
        ref = kvb.at[m, (ym, yp)[i], pl.ds(128 * i, 128)]
        return rcopy(ref, ref, k_ssem.at[m, 2 + i], k_rsem.at[m, 2 + i], (dyp, dym)[i])

    def kv_half_in(m, i):
        ref = kvb.at[m, y2, pl.ds(128 * i, 128)]
        return rcopy(ref, ref, k_ssem.at[m, 2 + i], k_rsem.at[m, 2 + i], sib)

    def rope(v, cos, sin):
        return v * cos + pltpu.roll(v, 64, 1) * sin

    def stage1(m):
        @pl.when(s > 0)
        def _():
            h_in(m).wait_recv()
            h_fwd(m).start()
            h_fwd_in(m).wait_recv()
            h_fwd(m).wait_send()

        h0 = hid[m, 0]
        h1 = hid[m, 1]
        f0, f1 = h0.astype(jnp.float32), h1.astype(jnp.float32)
        ms = jnp.sum(f0 * f0 + f1 * f1, axis=1, keepdims=True) * (1.0 / 2048.0)
        r = lax.rsqrt(ms + EPS)
        cos = cos_ref[m]
        sin = sin_ref[m]
        kv = jnp.dot(h0, wkv[0:4].reshape(HALF, KVC), preferred_element_type=jnp.float32)
        kv += jnp.dot(h1, wkv[4:8].reshape(HALF, KVC), preferred_element_type=jnp.float32)
        kv = kv * r
        for j in range(2):
            kvb[m, y, :, j * 128:(j + 1) * 128] = rope(kv[:, j * 128:(j + 1) * 128], cos, sin).astype(jnp.bfloat16)
        kvb[m, y, :, 256:512] = kv[:, 256:512].astype(jnp.bfloat16)
        kv_out(m, 0).start()
        kv_out(m, 1).start()
        rq = r * QSCALE
        for n in range(2):
            q = jnp.dot(h0, wq[0:4, :, :, n * 512:(n + 1) * 512].reshape(HALF, 512), preferred_element_type=jnp.float32)
            q += jnp.dot(h1, wq[4:8, :, :, n * 512:(n + 1) * 512].reshape(HALF, 512), preferred_element_type=jnp.float32)
            q = q * rq
            for j in range(4):
                h = n * 4 + j
                qb[m % 2, :, h * 128:(h + 1) * 128] = rope(q[:, j * 128:(j + 1) * 128], cos, sin).astype(jnp.bfloat16)
        for i in range(2):
            kv_in(m, i).wait_recv()
            kv_half(m, i).start()

    def attn_head(m, h):
        j = h // 4
        k = kvb[m, :, :, pl.ds(pl.multiple_of(j * 128, 128), 128)].reshape(4 * ROWS, HEAD_DIM)
        v = kvb[m, :, :, pl.ds(pl.multiple_of(256 + j * 128, 128), 128)].reshape(4 * ROWS, HEAD_DIM)
        at = pl.ds(pl.multiple_of(h * 128, 128), 128)
        q = qb[m % 2, :, at]
        sc = lax.dot_general(q, k, (((1,), (1,)), ((), ())), preferred_element_type=jnp.float32)
        sc = sc + bias[...]
        mx = jnp.max(sc, axis=1, keepdims=True)
        p = jnp.exp2(sc - mx)
        total = jnp.sum(p, axis=1, keepdims=True)
        o = jnp.dot(p.astype(jnp.bfloat16), v, preferred_element_type=jnp.float32)
        att[m, c, :, at] = (o / total).astype(jnp.bfloat16)

    def a_send(m, j):
        ref = att.at[m, c, :, j * 512:(j + 1) * 512]
        return rcopy(ref, ref, a_ssem.at[m, j], a_rsem.at[m, j], sib)

    def a_in(m, j):
        ref = att.at[m, 1 - c, :, j * 512:(j + 1) * 512]
        return rcopy(ref, ref, a_ssem.at[m, j], a_rsem.at[m, j], sib)

    def x_send(m):
        return rcopy(outb.at[m], hid.at[m, c], x_ssem.at[m], x_rsem.at[m, 0], xnext)

    out_cols = pl.ds(pl.multiple_of(c * HALF, HALF), HALF)
    out_cols_o = pl.ds(pl.multiple_of((1 - c) * HALF, HALF), HALF)

    def o_local(m):
        return pltpu.make_async_copy(outb.at[m, toks], out_ref.at[0, m, :, out_cols], lsem.at[4 + m])

    def o_sib(m):
        return rcopy(outb.at[m, toks_o], out_ref.at[0, m, :, out_cols], o_ssem.at[m], o_rsem.at[m], sib)

    def o_sib_in(m):
        ref = out_ref.at[0, m, :, out_cols_o]
        return rcopy(ref, ref, o_ssem.at[m], o_rsem.at[m], sib)

    def stage2(m):
        kp = kpos_ref[m]
        bias[...] = jnp.where((kp >= qbeg_ref[m]) & (kp <= qpos_ref[m]), 0.0, -1e30)
        for i in range(2):
            kv_half_in(m, i).wait_recv()
        for j in range(2):
            def head_pair(i, _):
                attn_head(m, j * 4 + i * 2)
                attn_head(m, j * 4 + i * 2 + 1)
                return 0
            lax.fori_loop(0, 2, head_pair, 0)
            a_send(m, j).start()
        for j in range(2):
            a_in(m, j).wait_recv()
        for n, w in enumerate((woa, wob)):
            o = jnp.dot(att[m, 0], w[0:4].reshape(HALF, 512), preferred_element_type=jnp.float32)
            o += jnp.dot(att[m, 1], w[4:8].reshape(HALF, 512), preferred_element_type=jnp.float32)
            o += hid[m, c, :, n * 512:(n + 1) * 512].astype(jnp.float32)
            outb[m, :, n * 512:(n + 1) * 512] = o.astype(jnp.bfloat16)

        @pl.when(s < SECTIONS - 1)
        def _():
            x_send(m).start()
        o_sib(m).start()
        o_local(m).start()

    def step(i, _):
        @pl.when(i < MICRO)
        def _():
            stage1(i)

        @pl.when(i > 0)
        def _():
            stage2(i - 1)
        return 0

    lax.fori_loop(0, MICRO + 1, step, 0)

    comm.drain()
    for m in range(MICRO):
        @pl.when(s < SECTIONS - 1)
        def _():
            x_send(m).wait_send()
        for i in range(2):
            kv_out(m, i).wait_send()
            kv_half(m, i).wait_send()
            a_send(m, i).wait_send()
        o_local(m).wait()
        o_sib(m).wait_send()
        o_sib_in(m).wait_recv()


def body(x_in, norm_gain, w_qkv, w_out, cycle_size, token_pos, doc_starts):
    cp = lax.axis_index("cp")
    chip = cp // 2
    gain = lax.dynamic_slice_in_dim(norm_gain[0], cp * 32, 32)
    wg = (w_qkv[0].astype(jnp.float32) * gain[:, None]).astype(jnp.bfloat16)
    wo = w_out[0]
    parts = []
    for c in range(2):
        parts.append(jnp.concatenate([
            wg[:, 2048 + 256 * c:2048 + 256 * (c + 1)], wg[:, 2560 + 256 * c:2560 + 256 * (c + 1)],
            wg[:, HALF * c:HALF * (c + 1)], wo[:, HALF * c:HALF * (c + 1)]], axis=1))
    wh = jnp.stack(parts)
    qpos = lax.dynamic_slice_in_dim(token_pos, chip * ROWS, ROWS, 1)
    kpos = lax.dynamic_slice_in_dim(token_pos, (cp // 8) * 4 * ROWS, 4 * ROWS, 1)
    starts = doc_starts[:, None, :]
    qbeg = jnp.max(jnp.where(starts <= qpos[:, :, None], starts, 0), axis=-1)
    inverse = jnp.power(jnp.float32(ROPE_BASE), -2.0 * jnp.arange(64, dtype=jnp.float32) / HEAD_DIM)
    angles = (qpos - qbeg).astype(jnp.float32)[:, :, None] * inverse[None, None, :]
    cos, sin = jnp.cos(angles), jnp.sin(angles)
    cos = jnp.concatenate([cos, cos], axis=-1)
    sin = jnp.concatenate([-sin, sin], axis=-1)
    vm = pl.BlockSpec(memory_space=pltpu.VMEM)
    anyspace = pl.BlockSpec(memory_space=pl.ANY)
    bf = jnp.bfloat16
    dma = pltpu.SemaphoreType.DMA
    return pl.pallas_call(
        kernel,
        name="relay",
        out_shape=jax.ShapeDtypeStruct((1, MICRO, 128, 2 * HALF), bf),
        in_specs=[vm, anyspace, vm, vm, vm, vm, vm],
        out_specs=anyspace,
        scratch_shapes=[
            pltpu.VMEM((NZ, NY, BLK, KVC), bf), pltpu.VMEM((NZ, NY, BLK, HALF), bf),
            pltpu.VMEM((NZ, NY, BLK, KVC), bf), pltpu.VMEM((NZ, NY, BLK, KVC), bf),
            pltpu.VMEM((MICRO, 2, ROWS, HALF), bf),
            pltpu.VMEM((MICRO, NY, ROWS, KVC), bf),
            pltpu.VMEM((2, ROWS, HALF), bf),
            pltpu.VMEM((MICRO, 2, ROWS, HALF), bf),
            pltpu.VMEM((MICRO, ROWS, HALF), bf),
            pltpu.VMEM((ROWS, 4 * ROWS), jnp.float32),
            dma((N_GATHER,)), dma((N_GATHER,)), dma((8,)),
            dma((MICRO,)), dma((MICRO, 2)), dma((MICRO, 2)), dma((MICRO, 2)),
            dma((MICRO, 4)), dma((MICRO, 4)), dma((MICRO, 2)), dma((MICRO, 2)), dma((MICRO,)), dma((MICRO,)),
        ],
        compiler_params=pltpu.CompilerParams(
            collective_id=0, has_side_effects=True, vmem_limit_bytes=60 * 1024 * 1024),
    )(wh, x_in, cos, sin, qpos[:, :, None], qbeg[:, :, None], kpos[:, None, :])


def solution(mesh):
    in_specs = (P(None, "cp", None), P("pp", None), P("pp", "cp", None), P("pp", "cp", None), P(), P(), P())
    return jax.shard_map(body, mesh=mesh, in_specs=in_specs, out_specs=P("pp", None, "cp", None), check_vma=False)
```

time: 684 us -> 321 us (0.47); the launches traced: 675 us -> 320 us
  waiting for transfers between devices: 409 us -> 0 us
  Pallas kernels: 0 us -> 304 us
  local copies, waits for them, and re-layouts: 105 us -> 9.59 us
  matrix products: 48.8 us -> 0 us
  other arithmetic: 50 us -> 6.77 us
  starting transfers between devices: 41.3 us -> 0 us
  between operations: 14.6 us -> 0.05 us
    pallas_call x0 -> x1, Pallas kernels: none -> 304 us  [body(): pl.pallas_call(kernel, name='relay', out_shape=jax.ShapeDtypeStruct((1, M...]
    ppermute x27 -> x0, waiting for transfers between devices: 297 us -> none  [the longest x6 155 us: from_behind(): lax.ppermute(value, axis, [(source, source + steps) for source in range(l...]
    all_gather x1 -> x0, waiting for transfers between devices: 112 us -> none  [side_by_side(): lax.all_gather(both, axis, axis=dim, tiled=True)]
    dot_general x16 -> x0, matrix products: 48.8 us -> none  [the longest x4 26 us: front_work(): projected = jnp.dot(normed, qkv_full, preferred_element_type=jnp.float32)]
    ppermute x27 -> x0, starting transfers between devices: 41.3 us -> none  [the longest x21 30.1 us: swapped(): lax.ppermute(array, axis, [(i, i ^ 1 << stride) for i in range(lax.axis_s...]
    select_n x6 -> x0, local copies, waits for them, and re-layouts: 28.5 us -> none  [collect_keys(): jnp.where(upper_half, jnp.concatenate([partner, key_block], axis=0), jnp....]
    select_n x43 -> x0, other arithmetic: 28 us -> none  [the longest x21 13.2 us: collect_keys(): jnp.where(upper_half, jnp.concatenate([partner, key_block], axis=0), jnp....]
    squeeze x3 -> x0, local copies, waits for them, and re-layouts: 16.2 us -> none  [the longest x1 8.29 us: body(): out_full = out_gathered[0]]
  transfers between devices with their start and end apart: 28 -> 0, of which waited for: 26 -> 0; matrix products, arithmetic and copies ran while one was open for 2% -> 0% of each run, Pallas kernels for 0% -> 0%
where the time goes in v1:
time: 321 us; the launch traced here: 320 us
  Pallas kernels  304 us (95%)
  local copies, waits for them, and re-layouts  9.59 us (3%)
  other arithmetic  6.77 us (2%)
    pallas_call x1, Pallas kernels, body(): pl.pallas_call(kernel, name='relay', out_shape=jax.ShapeDtypeStruct((1, M...  304 us

profile of v1, /device:TPU:7, one launch (start us, length us, event | category | flops | bytes accessed | tf_op | source)
XLA Modules:
  0.0 320.3 jit_solution(5421504678996359173)
XLA Ops:
  0.0 0.0 copy-start
  0.0 0.7 copy-done
  0.7 0.1 fusion.2
  0.8 0.7 fusion.6
  1.5 0.7 constant_dynamic-slice_fusion.1
  2.2 1.1 select_reduce_fusion
  3.2 0.7 subtract_convert_fusion
  3.9 0.7 constant_dynamic-slice_fusion
  4.6 0.6 broadcast_in_dim.27.kpos_ref
  5.3 0.9 fusion.5
  6.1 1.0 fusion
  7.2 0.7 pad_maximum_fusion.2.wh_ref
  8.0 1.0 copy.9.qpos_ref
  9.0 1.0 copy.10.qbeg_ref
  10.0 1.9 fusion.1
  11.9 1.3 pad_maximum_fusion
  13.2 303.9 %relay.1 = bf16[1,4,128,2048]{3,2,1,0:T(8,128)(2,1)} custom-call(bf16[2,32,2560]{2,1,0:T(8,128)(2,1)} %pad_maximum_fusion.2.wh_ref, bf16[4,128,2048]{2,1,0:T(8,128)(2,1)} %x_ref.1, f32[4,256,128]{2,1,0:T(8,128)} %get-tuple-element.18.cos_ref, f32[4,256,128]{2,1,0:T(8,128)} %get-tuple-element.19.sin_ref, s32[4,256,1]{2,1,0:T(8,128)} %copy.9.qpos_ref, ...), custom_call_target="tpu_custom_call" | custom-call | tf_op jit(solution)/shard_map/relay/pallas_call | solution.py:383
  317.2 3.2 copy.12
  (4 shorter events, 0.1 us)
Async XLA Ops:
  0.0 0.7 copy-start

commit v2 on v1

v2 whole, which is shorter than its diff:
```python
import functools
import math

import jax
import jax.numpy as jnp
from jax import lax
from jax.experimental import pallas as pl
from jax.experimental.pallas import tpu as pltpu
from jax.sharding import PartitionSpec as P

MESH = pl.DeviceIdType.MESH
HEAD_DIM = 128
MICRO = 4
SECTIONS = 4
NY = 4
NZ = 8
BLK = 64
ROWS = 256
HALF = 1024
KVC = 512
EPS = 1e-05
ROPE_BASE = 500000.0
QSCALE = HEAD_DIM ** (-0.5) * math.log2(math.e)
N_GATHER = 200
OAC = 640
OBC = 384
STEP = 128


class Comm:
    def __init__(self, ssem, rsem, home):
        self.ssem, self.rsem, self.home = ssem, rsem, home
        self.count = 0
        self.sent = []

    def make(self, src, dst, idx, dev):
        return pltpu.make_async_remote_copy(
            src_ref=src, dst_ref=dst, send_sem=self.ssem.at[idx], recv_sem=self.rsem.at[idx],
            device_id=dev, device_id_type=MESH)

    def send(self, ref, dev, dst=None):
        idx = self.count
        self.count += 1
        copy = self.make(ref, ref if dst is None else dst, idx, dev)
        copy.start()
        self.sent.append(copy)
        return idx

    def wait(self, ref, idx):
        self.make(ref, ref, idx, self.home).wait_recv()

    def drain(self):
        for copy in self.sent:
            copy.wait_send()
        self.sent = []


def kernel(wqkv_ref, wout_ref, gain_ref, pos_ref, doc_ref, inv_ref, x_ref, out_ref,
           wkv, wq0, wq1, woa, wob, stage, hid, kvb, qb, att, outb, cos_t, sin_t, qpos_t, qbeg_t, kpos_t,
           g_ssem, g_rsem, x_ssem, x_rsem, d_ssem, d_rsem, k_ssem, k_rsem, a_ssem, a_rsem, o_ssem, o_rsem, l_sem):
    s = lax.axis_index("pp")
    cp = lax.axis_index("cp")
    c = cp % 2
    chip = cp // 2
    y = chip % NY
    z = chip // NY
    ym, yp, y2 = (y + NY - 1) % NY, (y + 1) % NY, (y + 2) % NY

    def dev(yy, zz, cc):
        return (s, (zz * NY + yy) * 2 + cc)

    sib = dev(y, z, 1 - c)
    dyp, dym = dev(yp, z, c), dev(ym, z, c)
    dzp, dzm = dev(y, (z + 1) % NZ, c), dev(y, (z + NZ - 1) % NZ, c)
    xnext, xprev = ((s + 1) % SECTIONS, cp), ((s + SECTIONS - 1) % SECTIONS, cp)
    neighbours = (sib, dyp, dym, dzp, dzm, xnext, xprev)

    barrier = pltpu.get_barrier_semaphore()
    for d in neighbours:
        pl.semaphore_signal(barrier, inc=1, device_id=d, device_id_type=MESH)

    mine = pl.ds(pl.multiple_of(c * 32, 32), 32)
    other = pl.ds(pl.multiple_of((1 - c) * 32, 32), 32)
    toks = pl.ds(pl.multiple_of(c * STEP, STEP), STEP)
    toks_o = pl.ds(pl.multiple_of((1 - c) * STEP, STEP), STEP)

    def rcopy(src, dst, ss, rs, d):
        return pltpu.make_async_remote_copy(src_ref=src, dst_ref=dst, send_sem=ss, recv_sem=rs,
                                            device_id=d, device_id_type=MESH)

    def x_local(m, h):
        return pltpu.make_async_copy(x_ref.at[m, :, h * HALF:(h + 1) * HALF], hid.at[m, h, toks], x_rsem.at[m, h])

    def x_sib(m, h):
        return rcopy(hid.at[m, h, toks], hid.at[m, h, toks], d_ssem.at[m, h], d_rsem.at[m, h], sib)

    def x_sib_in(m, h):
        return rcopy(hid.at[m, h, toks_o], hid.at[m, h, toks_o], d_ssem.at[m, h], d_rsem.at[m, h], sib)

    @pl.when(s == 0)
    def _():
        for m in range(MICRO):
            for h in range(2):
                x_local(m, h).start()

    at128 = pl.ds(pl.multiple_of(cp // 4 * 128, 128), 128)
    g_row = jnp.broadcast_to(gain_ref[0:1, at128], (32, 128))
    lane = lax.broadcasted_iota(jnp.int32, (32, 128), 1)
    sub = lax.broadcasted_iota(jnp.int32, (32, 128), 0)
    g_col = jnp.sum(jnp.where(lane == sub + cp % 4 * 32, g_row, 0.0), axis=1, keepdims=True)
    for cc in range(2):
        for src_at, dst_at, n in ((2048 + 256 * cc, 0, 256), (2560 + 256 * cc, 256, 256), (HALF * cc, 512, HALF)):
            part = wqkv_ref[0, :, src_at:src_at + n].astype(jnp.float32) * g_col
            stage[cc, :, dst_at:dst_at + n] = part.astype(jnp.bfloat16)
        stage[cc, :, 1536:2560] = wout_ref[0, :, HALF * cc:HALF * (cc + 1)]
    cols = ((wkv, 0, 512), (wq0, 512, 512), (wq1, 1024, 512), (woa, 1536, OAC), (wob, 1536 + OAC, OBC))
    for w, at, n in cols:
        w[z, y, mine, :] = stage[c, :, at:at + n]

    pl.semaphore_wait(barrier, len(neighbours))

    comm = Comm(g_ssem, g_rsem, sib)
    sibs = {}
    for i in (1, 2, 0, 4, 3):
        w, at, n = cols[i]
        sibs[i] = comm.send(stage.at[1 - c, :, at:at + n], sib, dst=w.at[z, y, mine])

    def own_ready(i):
        comm.wait(cols[i][0].at[z, y, other], sibs[i])

    lo, hi, full = pl.ds(0, 32), pl.ds(32, 32), pl.ds(0, 64)

    class ZthenY:
        def __init__(self, w):
            self.w = w
            self.y_sent, self.half = {}, []

        def send_z(self):
            own = self.w.at[z, y]
            self.p, self.m = comm.send(own, dzp), comm.send(own, dzm)

        def send_y(self, key):
            blk = self.w.at[(z + NZ + key) % NZ, y]
            self.y_sent[key] = (comm.send(blk, dyp), comm.send(blk, dym))

        def ring(self, d, with_y):
            w, zm, zp = self.w, (z + NZ - d) % NZ, (z + d) % NZ
            if d == 4:
                comm.wait(w.at[zp, y, lo], self.p)
                comm.wait(w.at[zp, y, hi], self.m)
                if with_y:
                    self.send_y(4)
                return
            comm.wait(w.at[zm, y], self.p)
            self.p = comm.send(w.at[zm, y, lo if d == 3 else full], dzp)
            if with_y:
                self.send_y(-d)
            comm.wait(w.at[zp, y], self.m)
            self.m = comm.send(w.at[zp, y, hi if d == 3 else full], dzm)
            if with_y:
                self.send_y(d)

        def arrive(self, *keys):
            for key in keys:
                zz = (z + NZ + key) % NZ
                i_p, i_m = self.y_sent[key]
                comm.wait(self.w.at[zz, ym], i_p)
                h_p = comm.send(self.w.at[zz, ym, lo], dyp)
                comm.wait(self.w.at[zz, yp], i_m)
                h_m = comm.send(self.w.at[zz, yp, hi], dym)
                self.half.append((zz, h_p, h_m))

        def finish(self):
            for zz, h_p, h_m in self.half:
                comm.wait(self.w.at[zz, y2, lo], h_p)
                comm.wait(self.w.at[zz, y2, hi], h_m)

    class YthenZ:
        def __init__(self, w):
            self.w = w
            self.at = {}

        def send_y(self):
            own = self.w.at[z, y]
            self.p, self.m = comm.send(own, dyp), comm.send(own, dym)

        def y_forward(self):
            w = self.w
            comm.wait(w.at[z, ym], self.p)
            self.p = comm.send(w.at[z, ym, lo], dyp)
            comm.wait(w.at[z, yp], self.m)
            self.m = comm.send(w.at[z, yp, hi], dym)

        def y_finish(self):
            comm.wait(self.w.at[z, y2, lo], self.p)
            comm.wait(self.w.at[z, y2, hi], self.m)

        def send_z(self, *ks):
            for k in ks:
                blk = self.w.at[z, (y, ym, yp, y2)[k]]
                self.at[k] = (comm.send(blk, dzp), comm.send(blk, dzm))

        def ring(self, d):
            w, zm, zp = self.w, (z + NZ - d) % NZ, (z + d) % NZ
            for k in range(4):
                yy = (y, ym, yp, y2)[k]
                p, m = self.at[k]
                if d == 4:
                    comm.wait(w.at[zp, yy, lo], p)
                    comm.wait(w.at[zp, yy, hi], m)
                    continue
                comm.wait(w.at[zm, yy], p)
                p = comm.send(w.at[zm, yy, lo if d == 3 else full], dzp)
                comm.wait(w.at[zp, yy], m)
                m = comm.send(w.at[zp, yy, hi if d == 3 else full], dzm)
                self.at[k] = (p, m)

    eye = lax.broadcasted_iota(jnp.int32, (STEP, STEP), 0) == lax.broadcasted_iota(jnp.int32, (STEP, STEP), 1)
    sign = jnp.where(lax.broadcasted_iota(jnp.int32, (1, HEAD_DIM), 1) < 64, -1.0, 1.0)

    def table(m):
        starts = jnp.broadcast_to(doc_ref[m:m + 1, :].astype(jnp.float32), (STEP, 128))
        for b in range(2):
            rows = slice(b * STEP, (b + 1) * STEP)
            at = pl.ds(pl.multiple_of(chip * ROWS + b * STEP, STEP), STEP)
            row = jnp.broadcast_to(pos_ref[m:m + 1, at].astype(jnp.float32), (STEP, STEP))
            pos = jnp.sum(jnp.where(eye, row, 0.0), axis=1, keepdims=True)
            beg = jnp.max(jnp.where(starts <= pos, starts, 0.0), axis=1, keepdims=True)
            angles = (pos - beg) * inv_ref[...]
            cos_t[m, rows, :] = jnp.cos(angles)
            sin_t[m, rows, :] = jnp.sin(angles) * sign
            qpos_t[m, rows, :] = jnp.broadcast_to(pos, (STEP, 128))
            qbeg_t[m, rows, :] = jnp.broadcast_to(beg, (STEP, 128))
        kpos_t[m] = pos_ref[m:m + 1, pl.ds(pl.multiple_of(z * 4 * ROWS, 4 * ROWS), 4 * ROWS)].astype(jnp.float32)

    def half_rows(r):
        return pl.ds(pl.multiple_of(r * STEP, STEP), STEP)

    def h_in(m, r):
        ref = hid.at[m, c, half_rows(r)]
        return rcopy(ref, ref, x_ssem.at[m, r], x_rsem.at[m, r], xprev)

    def h_fwd(m, r):
        ref = hid.at[m, c, half_rows(r)]
        return rcopy(ref, ref, d_ssem.at[m, r], d_rsem.at[m, r], sib)

    def h_fwd_in(m, r):
        ref = hid.at[m, 1 - c, half_rows(r)]
        return rcopy(ref, ref, d_ssem.at[m, r], d_rsem.at[m, r], sib)

    def kv_out(m, r, i):
        ref = kvb.at[m, y, half_rows(r)]
        return rcopy(ref, ref, k_ssem.at[m, r, i], k_rsem.at[m, r, i], (dyp, dym)[i])

    def kv_in(m, r, i):
        ref = kvb.at[m, (ym, yp)[i], half_rows(r)]
        return rcopy(ref, ref, k_ssem.at[m, r, i], k_rsem.at[m, r, i], sib)

    def quarter(r, i):
        return pl.ds(pl.multiple_of(r * STEP + i * 64, 64), 64)

    def kv_half(m, r, i):
        ref = kvb.at[m, (ym, yp)[i], quarter(r, i)]
        return rcopy(ref, ref, k_ssem.at[m, r, 2 + i], k_rsem.at[m, r, 2 + i], (dyp, dym)[i])

    def kv_half_in(m, r, i):
        ref = kvb.at[m, y2, quarter(r, i)]
        return rcopy(ref, ref, k_ssem.at[m, r, 2 + i], k_rsem.at[m, r, 2 + i], sib)

    def rope(v, cos, sin):
        return v * cos + pltpu.roll(v, 64, 1) * sin

    def hin(m, r):
        @pl.when(s > 0)
        def _():
            with jax.named_scope("hin"):
                h_in(m, r).wait_recv()
            h_fwd(m, r).start()

    def front(m, r):
        @pl.when(s > 0)
        def _():
            with jax.named_scope("hfwd"):
                h_fwd_in(m, r).wait_recv()

        with jax.named_scope("front"):
            rows = half_rows(r)
            h0 = hid[m, 0, rows]
            h1 = hid[m, 1, rows]
            f0, f1 = h0.astype(jnp.float32), h1.astype(jnp.float32)
            ms = jnp.sum(f0 * f0 + f1 * f1, axis=1, keepdims=True) * (1.0 / (2 * HALF))
            scale = lax.rsqrt(ms + EPS)
            cos = cos_t[m, rows]
            sin = sin_t[m, rows]
            kv = jnp.dot(h0, wkv[0:4].reshape(HALF, KVC), preferred_element_type=jnp.float32)
            kv += jnp.dot(h1, wkv[4:8].reshape(HALF, KVC), preferred_element_type=jnp.float32)
            kv = kv * scale
            for j in range(2):
                kvb[m, y, rows, j * 128:(j + 1) * 128] = rope(kv[:, j * 128:(j + 1) * 128], cos, sin).astype(jnp.bfloat16)
            kvb[m, y, rows, 256:512] = kv[:, 256:512].astype(jnp.bfloat16)
            kv_out(m, r, 0).start()
            kv_out(m, r, 1).start()
            scale = scale * QSCALE
            for n, w in enumerate((wq0, wq1)):
                q = jnp.dot(h0, w[0:4].reshape(HALF, 512), preferred_element_type=jnp.float32)
                q += jnp.dot(h1, w[4:8].reshape(HALF, 512), preferred_element_type=jnp.float32)
                q = q * scale
                for j in range(4):
                    h = n * 4 + j
                    qb[m, rows, h * 128:(h + 1) * 128] = rope(q[:, j * 128:(j + 1) * 128], cos, sin).astype(jnp.bfloat16)

    def kv_forward(m, r):
        with jax.named_scope("kvin"):
            for i in range(2):
                kv_in(m, r, i).wait_recv()
                kv_half(m, r, i).start()

    def a_send(m, r):
        ref = att.at[m, c, half_rows(r)]
        return rcopy(ref, ref, a_ssem.at[m, r], a_rsem.at[m, r], sib)

    def a_in(m, r):
        ref = att.at[m, 1 - c, half_rows(r)]
        return rcopy(ref, ref, a_ssem.at[m, r], a_rsem.at[m, r], sib)

    def x_send(m, r):
        return rcopy(outb.at[m, half_rows(r)], hid.at[m, c, half_rows(r)], x_ssem.at[m, r], x_rsem.at[m, r], xnext)

    out_cols = pl.ds(pl.multiple_of(c * HALF, HALF), HALF)
    out_cols_o = pl.ds(pl.multiple_of((1 - c) * HALF, HALF), HALF)

    def o_local(m):
        return pltpu.make_async_copy(outb.at[m, toks], out_ref.at[0, m, :, out_cols], l_sem.at[m])

    def o_sib(m):
        return rcopy(outb.at[m, toks_o], out_ref.at[0, m, :, out_cols], o_ssem.at[m], o_rsem.at[m], sib)

    def o_sib_in(m):
        ref = out_ref.at[0, m, :, out_cols_o]
        return rcopy(ref, ref, o_ssem.at[m], o_rsem.at[m], sib)

    def attend(m, r):
        with jax.named_scope("attn"):
            rows = half_rows(r)
            kp = kpos_t[m]
            bias = jnp.where((kp >= qbeg_t[m, rows, 0:1]) & (kp <= qpos_t[m, rows, 0:1]), 0.0, -1e30)
            ones = jnp.ones((4 * ROWS, HEAD_DIM), jnp.bfloat16)
            for h in range(8):
                j = h // 4
                k = kvb[m, :, :, j * 128:(j + 1) * 128].reshape(4 * ROWS, HEAD_DIM)
                v = kvb[m, :, :, 256 + j * 128:256 + (j + 1) * 128].reshape(4 * ROWS, HEAD_DIM)
                v = jnp.concatenate([v, ones], axis=1)
                q = qb[m, rows, h * 128:(h + 1) * 128]
                sc = lax.dot_general(q, k, (((1,), (1,)), ((), ())), preferred_element_type=jnp.float32) + bias
                mx = jnp.max(sc, axis=1, keepdims=True)
                p = jnp.exp2(sc - mx)
                o = jnp.dot(p.astype(jnp.bfloat16), v, preferred_element_type=jnp.float32)
                att[m, c, rows, h * 128:(h + 1) * 128] = (o[:, :128] / o[:, 128:]).astype(jnp.bfloat16)
            a_send(m, r).start()

    def project(m, r):
        with jax.named_scope("ain"):
            a_in(m, r).wait_recv()
        with jax.named_scope("outp"):
            rows = half_rows(r)
            for w, at, n in ((woa, 0, OAC), (wob, OAC, OBC)):
                o = jnp.dot(att[m, 0, rows], w[0:4].reshape(HALF, n), preferred_element_type=jnp.float32)
                o += jnp.dot(att[m, 1, rows], w[4:8].reshape(HALF, n), preferred_element_type=jnp.float32)
                o += hid[m, c, rows, at:at + n].astype(jnp.float32)
                outb[m, rows, at:at + n] = o.astype(jnp.bfloat16)

            @pl.when(s < SECTIONS - 1)
            def _():
                x_send(m, r).start()

            @pl.when(c != r)
            def _():
                o_sib(m).start()

            @pl.when(c == r)
            def _():
                o_local(m).start()

    first_section = s == 0
    q0_, q1_, kv_, oa_, ob_ = ZthenY(wq0), ZthenY(wq1), YthenZ(wkv), YthenZ(woa), ZthenY(wob)
    qs = (q0_, q1_)
    with jax.named_scope("flood1"):
        for i, q_ in ((1, q0_), (2, q1_)):
            own_ready(i)
            q_.send_z()
            q_.send_y(0)
        own_ready(0)
        kv_.send_y()
        own_ready(4)
        ob_.send_z()
        ob_.send_y(0)
        own_ready(3)
        oa_.send_y()
    table(0)

    @pl.when(first_section)
    def _():
        for m in range(MICRO):
            for h in range(2):
                x_local(m, h).wait()
                x_sib(m, h).start()

    def all_q(step, *args):
        for q_ in qs:
            getattr(q_, step)(*args)

    with jax.named_scope("flood2"):
        all_q("ring", 1, True)
        kv_.y_forward()
        ob_.ring(1, False)
        all_q("arrive", 0)
    with jax.named_scope("flood3"):
        all_q("ring", 2, True)
        ob_.ring(2, False)
        kv_.y_finish()
        all_q("arrive", -1, 1)
    with jax.named_scope("flood4"):
        all_q("ring", 3, True)
        kv_.send_z(0, 1, 2, 3)
        ob_.ring(3, False)
        all_q("ring", 4, True)
        ob_.ring(4, False)
        all_q("arrive", -2, 2)
        oa_.y_forward()
    table(1)
    with jax.named_scope("flood5"):
        kv_.ring(1)
        all_q("arrive", -3, 3)
    table(2)
    with jax.named_scope("flood6"):
        kv_.ring(2)
        for key in (-1, 1, -2, 2):
            ob_.send_y(key)
        all_q("arrive", 4)
        oa_.y_finish()
    table(3)
    with jax.named_scope("flood7"):
        kv_.ring(3)
        oa_.send_z(0, 1, 2, 3)
        kv_.ring(4)
        all_q("finish")

    @pl.when(first_section)
    def _():
        for m in range(MICRO):
            for h in range(2):
                x_sib_in(m, h).wait_recv()
        front(0, 0)

    with jax.named_scope("flood8"):
        for key in (-3, 3, 4):
            ob_.send_y(key)
        ob_.arrive(0, -1, 1)
        oa_.ring(1)

    @pl.when(first_section)
    def _():
        front(0, 1)

    with jax.named_scope("flood9"):
        ob_.arrive(-2, 2)
        oa_.ring(2)

    @pl.when(first_section)
    def _():
        kv_forward(0, 0)

    with jax.named_scope("flood10"):
        ob_.arrive(-3, 3, 4)
        oa_.ring(3)

    @pl.when(first_section)
    def _():
        kv_forward(0, 1)
        front(1, 0)

    with jax.named_scope("flood11"):
        oa_.ring(4)
        ob_.finish()

    @pl.when(first_section)
    def _():
        front(1, 1)
        kv_forward(1, 0)

    @pl.when(s > 0)
    def _():
        def first(r, _):
            hin(0, r)
            front(0, r)
            return 0
        lax.fori_loop(0, 2, first, 0)
        kv_forward(0, 0)

    ahead = jnp.where(first_section, 1, 0)

    def step(m, _):
        late = m + ahead
        new = late + 1

        @pl.when(late < MICRO)
        def _():
            kv_forward(late, 1)

        @pl.when(new < MICRO)
        def _():
            hin(new, 0)
            front(new, 0)
        with jax.named_scope("kvh"):
            for r in range(2):
                for i in range(2):
                    kv_half_in(m, r, i).wait_recv()
        attend(m, 0)

        @pl.when(new < MICRO)
        def _():
            hin(new, 1)
        project(m, 0)

        @pl.when(new < MICRO)
        def _():
            front(new, 1)
        attend(m, 1)

        @pl.when(new < MICRO)
        def _():
            kv_forward(new, 0)
        project(m, 1)
        return 0

    lax.fori_loop(0, MICRO, step, 0)

    with jax.named_scope("drain"):
        comm.drain()

        def settle(m, _):
            for r in range(2):
                @pl.when(s < SECTIONS - 1)
                def _():
                    x_send(m, r).wait_send()
                h_fwd(m, r).wait_send()
                for i in range(2):
                    kv_out(m, r, i).wait_send()
                    kv_half(m, r, i).wait_send()
                a_send(m, r).wait_send()
            o_local(m).wait()
            o_sib(m).wait_send()
            o_sib_in(m).wait_recv()
            return 0
        lax.fori_loop(0, MICRO, settle, 0)


def body(x_in, norm_gain, w_qkv, w_out, cycle_size, token_pos, doc_starts):
    inverse = jnp.power(jnp.float32(ROPE_BASE), -2.0 * jnp.arange(64, dtype=jnp.float32) / HEAD_DIM)
    inverse = jnp.concatenate([inverse, inverse])[None, :]
    vm = pl.BlockSpec(memory_space=pltpu.VMEM)
    anyspace = pl.BlockSpec(memory_space=pl.ANY)
    bf, f32 = jnp.bfloat16, jnp.float32
    dma = pltpu.SemaphoreType.DMA
    return pl.pallas_call(
        kernel,
        name="relay",
        out_shape=jax.ShapeDtypeStruct((1, MICRO, 128, 2 * HALF), bf),
        in_specs=[vm, vm, vm, vm, vm, vm, anyspace],
        out_specs=anyspace,
        scratch_shapes=[
            pltpu.VMEM((NZ, NY, BLK, KVC), bf), pltpu.VMEM((NZ, NY, BLK, 512), bf), pltpu.VMEM((NZ, NY, BLK, 512), bf),
            pltpu.VMEM((NZ, NY, BLK, OAC), bf), pltpu.VMEM((NZ, NY, BLK, OBC), bf),
            pltpu.VMEM((2, 32, 2560), bf),
            pltpu.VMEM((MICRO, 2, ROWS, HALF), bf),
            pltpu.VMEM((MICRO, NY, ROWS, KVC), bf),
            pltpu.VMEM((MICRO, ROWS, HALF), bf),
            pltpu.VMEM((MICRO, 2, ROWS, HALF), bf),
            pltpu.VMEM((MICRO, ROWS, HALF), bf),
            pltpu.VMEM((MICRO, ROWS, 128), f32), pltpu.VMEM((MICRO, ROWS, 128), f32),
            pltpu.VMEM((MICRO, ROWS, 128), f32), pltpu.VMEM((MICRO, ROWS, 128), f32),
            pltpu.VMEM((MICRO, 1, 4 * ROWS), f32),
            dma((N_GATHER,)), dma((N_GATHER,)),
            dma((MICRO, 2)), dma((MICRO, 2)), dma((MICRO, 2)), dma((MICRO, 2)),
            dma((MICRO, 2, 4)), dma((MICRO, 2, 4)), dma((MICRO, 2)), dma((MICRO, 2)),
            dma((MICRO,)), dma((MICRO,)), dma((MICRO,)),
        ],
        compiler_params=pltpu.CompilerParams(
            collective_id=0, has_side_effects=True, vmem_limit_bytes=60 * 1024 * 1024),
    )(w_qkv, w_out, norm_gain, token_pos, doc_starts, inverse, x_in)


def solution(mesh):
    in_specs = (P(None, "cp", None), P("pp", None), P("pp", "cp", None), P("pp", "cp", None), P(), P(), P())
    return jax.shard_map(body, mesh=mesh, in_specs=in_specs, out_specs=P("pp", None, "cp", None), check_vma=False)
```

time: 321 us -> 228 us (0.71)
  Pallas kernels: 304 us -> 224 us
  local copies, waits for them, and re-layouts: 9.59 us -> 3.16 us
  other arithmetic: 6.77 us -> 0.6 us
    pallas_call x1, Pallas kernels: 304 us -> 224 us  [body(): pl.pallas_call(kernel, name='relay', out_shape=jax.ShapeDtypeStruct((1, M...]
    broadcast_in_dim x4 -> x0, local copies, waits for them, and re-layouts: 3.36 us -> none  [the longest x2 1.73 us: body(): qbeg = jnp.max(jnp.where(starts <= qpos[:, :, None], starts, 0), axis=-1)]
where the time goes in v2:
time: 228 us; the launch traced here: 227 us
  Pallas kernels  224 us (98%)
  local copies, waits for them, and re-layouts  3.16 us (1%)
    pallas_call x1, Pallas kernels, body(): pl.pallas_call(kernel, name='relay', out_shape=jax.ShapeDtypeStruct((1, M...  224 us

profile of v2, /device:TPU:7, one launch (start us, length us, event | category | flops | bytes accessed | tf_op | source)
XLA Modules:
  0.0 227.5 jit_solution(11391156322661227490)
XLA Ops:
  0.0 0.6 maximum_bitcast_fusion.inv_ref
  0.6 223.7 %relay.1 = bf16[1,4,128,2048]{3,2,1,0:T(8,128)(2,1)} custom-call(bf16[1,32,3072]{2,1,0:T(8,128)(2,1)} %wqkv_ref.1, bf16[1,32,2048]{2,1,0:T(8,128)(2,1)} %wout_ref.1, f32[1,2048]{1,0:T(1,128)} %gain_ref.1, s32[4,8192]{1,0:T(4,128)} %pos_ref.1, s32[4,128]{1,0:T(4,128)} %doc_ref.1, f32[1,128]{1,0:T(1,128)} %maximum_bitcast_fusion.inv_ref, ...), custom_call_target="tpu_custom_call" | custom-call | tf_op jit(solution)/shard_map/relay/pallas_call | solution.py:565
  224.3 3.2 %copy.8 = bf16[1,4,128,2048]{3,2,1,0:T(8,128)(2,1)} copy(bf16[1,4,128,2048]{3,2,1,0:T(8,128)(2,1)} %relay.1) | data formatting | bytes 4194304
  (1 shorter events, 0.0 us)

commit v3 on v2

--- a/solution.py
+++ b/solution.py
@@ -21,7 +21,8 @@
 EPS = 1e-05
 ROPE_BASE = 500000.0
 QSCALE = HEAD_DIM ** (-0.5) * math.log2(math.e)
-N_GATHER = 200
+N_GATHER = 197
+N_SEND = 40
 OAC = 640
 OBC = 384
 STEP = 128
@@ -35,12 +36,14 @@
 
     def make(self, src, dst, idx, dev):
         return pltpu.make_async_remote_copy(
-            src_ref=src, dst_ref=dst, send_sem=self.ssem.at[idx], recv_sem=self.rsem.at[idx],
+            src_ref=src, dst_ref=dst, send_sem=self.ssem.at[idx % N_SEND], recv_sem=self.rsem.at[idx],
             device_id=dev, device_id_type=MESH)
 
     def send(self, ref, dev, dst=None):
         idx = self.count
         self.count += 1
+        if idx >= N_SEND:
+            self.sent[idx - N_SEND].wait_send()
         copy = self.make(ref, ref if dst is None else dst, idx, dev)
         copy.start()
         self.sent.append(copy)
@@ -50,7 +53,7 @@
         self.make(ref, ref, idx, self.home).wait_recv()
 
     def drain(self):
-        for copy in self.sent:
+        for copy in self.sent[-N_SEND:]:
             copy.wait_send()
         self.sent = []
 
@@ -103,6 +106,8 @@
             for h in range(2):
                 x_local(m, h).start()
 
+    scope_a = jax.named_scope('stage')
+    scope_a.__enter__()
     at128 = pl.ds(pl.multiple_of(cp // 4 * 128, 128), 128)
     g_row = jnp.broadcast_to(gain_ref[0:1, at128], (32, 128))
     lane = lax.broadcasted_iota(jnp.int32, (32, 128), 1)
@@ -117,7 +122,9 @@
     for w, at, n in cols:
         w[z, y, mine, :] = stage[c, :, at:at + n]
 
-    pl.semaphore_wait(barrier, len(neighbours))
+    scope_a.__exit__(None, None, None)
+    with jax.named_scope('barrier'):
+        pl.semaphore_wait(barrier, len(neighbours))
 
     comm = Comm(g_ssem, g_rsem, sib)
     sibs = {}
@@ -200,9 +207,9 @@
                 blk = self.w.at[z, (y, ym, yp, y2)[k]]
                 self.at[k] = (comm.send(blk, dzp), comm.send(blk, dzm))
 
-        def ring(self, d):
+        def ring(self, d, *ks):
             w, zm, zp = self.w, (z + NZ - d) % NZ, (z + d) % NZ
-            for k in range(4):
+            for k in ks:
                 yy = (y, ym, yp, y2)[k]
                 p, m = self.at[k]
                 if d == 4:
@@ -248,24 +255,26 @@
         ref = hid.at[m, 1 - c, half_rows(r)]
         return rcopy(ref, ref, d_ssem.at[m, r], d_rsem.at[m, r], sib)
 
-    def kv_out(m, r, i):
-        ref = kvb.at[m, y, half_rows(r)]
-        return rcopy(ref, ref, k_ssem.at[m, r, i], k_rsem.at[m, r, i], (dyp, dym)[i])
-
-    def kv_in(m, r, i):
-        ref = kvb.at[m, (ym, yp)[i], half_rows(r)]
-        return rcopy(ref, ref, k_ssem.at[m, r, i], k_rsem.at[m, r, i], sib)
-
     def quarter(r, i):
         return pl.ds(pl.multiple_of(r * STEP + i * 64, 64), 64)
 
+    def kv_out(m, r, i, piece):
+        ref = kvb.at[m, y, quarter(r, i if piece == 0 else 1 - i)]
+        k = 2 * i + piece
+        return rcopy(ref, ref, k_ssem.at[r, k], k_rsem.at[m, r, k], (dyp, dym)[i])
+
+    def kv_in(m, r, i, piece):
+        ref = kvb.at[m, (ym, yp)[i], quarter(r, i if piece == 0 else 1 - i)]
+        k = 2 * i + piece
+        return rcopy(ref, ref, k_ssem.at[r, k], k_rsem.at[m, r, k], sib)
+
     def kv_half(m, r, i):
         ref = kvb.at[m, (ym, yp)[i], quarter(r, i)]
-        return rcopy(ref, ref, k_ssem.at[m, r, 2 + i], k_rsem.at[m, r, 2 + i], (dyp, dym)[i])
+        return rcopy(ref, ref, k_ssem.at[r, 4 + i], k_rsem.at[m, r, 4 + i], (dyp, dym)[i])
 
     def kv_half_in(m, r, i):
         ref = kvb.at[m, y2, quarter(r, i)]
-        return rcopy(ref, ref, k_ssem.at[m, r, 2 + i], k_rsem.at[m, r, 2 + i], sib)
+        return rcopy(ref, ref, k_ssem.at[r, 4 + i], k_rsem.at[m, r, 4 + i], sib)
 
     def rope(v, cos, sin):
         return v * cos + pltpu.roll(v, 64, 1) * sin
@@ -278,6 +287,7 @@
             h_fwd(m, r).start()
 
     def front(m, r):
+        m = jnp.asarray(m, jnp.int32)
         @pl.when(s > 0)
         def _():
             with jax.named_scope("hfwd"):
@@ -298,8 +308,14 @@
             for j in range(2):
                 kvb[m, y, rows, j * 128:(j + 1) * 128] = rope(kv[:, j * 128:(j + 1) * 128], cos, sin).astype(jnp.bfloat16)
             kvb[m, y, rows, 256:512] = kv[:, 256:512].astype(jnp.bfloat16)
-            kv_out(m, r, 0).start()
-            kv_out(m, r, 1).start()
+            @pl.when(m > 0)
+            def _():
+                for i in range(2):
+                    for piece in range(2):
+                        kv_out(m - 1, r, i, piece).wait_send()
+            for piece in range(2):
+                for i in range(2):
+                    kv_out(m, r, i, piece).start()
             scale = scale * QSCALE
             for n, w in enumerate((wq0, wq1)):
                 q = jnp.dot(h0, w[0:4].reshape(HALF, 512), preferred_element_type=jnp.float32)
@@ -310,10 +326,21 @@
                     qb[m, rows, h * 128:(h + 1) * 128] = rope(q[:, j * 128:(j + 1) * 128], cos, sin).astype(jnp.bfloat16)
 
     def kv_forward(m, r):
+        m = jnp.asarray(m, jnp.int32)
         with jax.named_scope("kvin"):
             for i in range(2):
-                kv_in(m, r, i).wait_recv()
+                kv_in(m, r, i, 0).wait_recv()
+
+                @pl.when(m > 0)
+                def _():
+                    kv_half(m - 1, r, i).wait_send()
                 kv_half(m, r, i).start()
+
+    def kv_wait(m):
+        for r in range(2):
+            for i in range(2):
+                kv_in(m, r, i, 1).wait_recv()
+                kv_half_in(m, r, i).wait_recv()
 
     def a_send(m, r):
         ref = att.at[m, c, half_rows(r)]
@@ -384,6 +411,10 @@
     first_section = s == 0
     q0_, q1_, kv_, oa_, ob_ = ZthenY(wq0), ZthenY(wq1), YthenZ(wkv), YthenZ(woa), ZthenY(wob)
     qs = (q0_, q1_)
+    def all_q(step, *args):
+        for q_ in qs:
+            getattr(q_, step)(*args)
+
     with jax.named_scope("flood1"):
         for i, q_ in ((1, q0_), (2, q1_)):
             own_ready(i)
@@ -391,6 +422,7 @@
             q_.send_y(0)
         own_ready(0)
         kv_.send_y()
+        kv_.send_z(0)
         own_ready(4)
         ob_.send_z()
         ob_.send_y(0)
@@ -405,116 +437,133 @@
                 x_local(m, h).wait()
                 x_sib(m, h).start()
 
-    def all_q(step, *args):
-        for q_ in qs:
-            getattr(q_, step)(*args)
-
     with jax.named_scope("flood2"):
         all_q("ring", 1, True)
+        kv_.ring(1, 0)
         kv_.y_forward()
+        kv_.send_z(1, 2)
         ob_.ring(1, False)
         all_q("arrive", 0)
     with jax.named_scope("flood3"):
         all_q("ring", 2, True)
+        kv_.ring(2, 0)
+        kv_.ring(1, 1, 2)
         ob_.ring(2, False)
         kv_.y_finish()
+        kv_.send_z(3)
         all_q("arrive", -1, 1)
     with jax.named_scope("flood4"):
         all_q("ring", 3, True)
-        kv_.send_z(0, 1, 2, 3)
+        kv_.ring(3, 0)
+        kv_.ring(2, 1, 2)
+        kv_.ring(1, 3)
         ob_.ring(3, False)
-        all_q("ring", 4, True)
-        ob_.ring(4, False)
         all_q("arrive", -2, 2)
-        oa_.y_forward()
     table(1)
     with jax.named_scope("flood5"):
-        kv_.ring(1)
+        all_q("ring", 4, True)
+        kv_.ring(4, 0)
+        kv_.ring(3, 1, 2)
+        kv_.ring(2, 3)
+        ob_.ring(4, False)
+        oa_.y_forward()
+        oa_.send_z(0, 1)
         all_q("arrive", -3, 3)
     table(2)
     with jax.named_scope("flood6"):
-        kv_.ring(2)
-        for key in (-1, 1, -2, 2):
-            ob_.send_y(key)
+        kv_.ring(4, 1, 2)
+        kv_.ring(3, 3)
+        oa_.ring(1, 0, 1)
+        oa_.y_finish()
+        oa_.send_z(2, 3)
         all_q("arrive", 4)
-        oa_.y_finish()
-    table(3)
-    with jax.named_scope("flood7"):
-        kv_.ring(3)
-        oa_.send_z(0, 1, 2, 3)
-        kv_.ring(4)
+        kv_.ring(4, 3)
         all_q("finish")
+
+    def each_half(*steps):
+        def both(r, _):
+            for one in steps:
+                one(r)
+            return 0
+        lax.fori_loop(0, 2, both, 0)
 
     @pl.when(first_section)
     def _():
         for m in range(MICRO):
             for h in range(2):
                 x_sib_in(m, h).wait_recv()
-        front(0, 0)
+        each_half(lambda r: front(0, r))
+
+    with jax.named_scope("flood7"):
+        for key in (-1, 1):
+            ob_.send_y(key)
+        oa_.ring(2, 0, 1)
+        oa_.ring(1, 2, 3)
+
+    @pl.when(first_section)
+    def _():
+        kv_forward(0, 0)
 
     with jax.named_scope("flood8"):
+        for key in (-2, 2):
+            ob_.send_y(key)
+        ob_.arrive(0, -1, 1)
+        oa_.ring(3, 0, 1)
+
+    @pl.when(first_section)
+    def _():
+        kv_forward(0, 1)
+
+    table(3)
+    with jax.named_scope("flood9"):
         for key in (-3, 3, 4):
             ob_.send_y(key)
-        ob_.arrive(0, -1, 1)
-        oa_.ring(1)
+        oa_.ring(2, 2, 3)
+        ob_.arrive(-2, 2)
+        oa_.ring(4, 0, 1)
 
     @pl.when(first_section)
     def _():
-        front(0, 1)
-
-    with jax.named_scope("flood9"):
-        ob_.arrive(-2, 2)
-        oa_.ring(2)
-
-    @pl.when(first_section)
-    def _():
-        kv_forward(0, 0)
+        with jax.named_scope("kvh"):
+            kv_wait(0)
+        attend(0, 0)
 
     with jax.named_scope("flood10"):
         ob_.arrive(-3, 3, 4)
-        oa_.ring(3)
+        oa_.ring(3, 2, 3)
 
     @pl.when(first_section)
     def _():
+        attend(0, 1)
+        front(1, 0)
+
+    with jax.named_scope("flood11"):
+        oa_.ring(4, 2, 3)
+        ob_.finish()
+
+    @pl.when(first_section)
+    def _():
+        project(0, 0)
+        front(1, 1)
+        project(0, 1)
+        kv_forward(1, 0)
+        kv_forward(1, 1)
+
+    @pl.when(s > 0)
+    def _():
+        each_half(lambda r: hin(0, r), lambda r: front(0, r))
+        kv_forward(0, 0)
         kv_forward(0, 1)
-        front(1, 0)
-
-    with jax.named_scope("flood11"):
-        oa_.ring(4)
-        ob_.finish()
-
-    @pl.when(first_section)
-    def _():
-        front(1, 1)
-        kv_forward(1, 0)
-
-    @pl.when(s > 0)
-    def _():
-        def first(r, _):
-            hin(0, r)
-            front(0, r)
-            return 0
-        lax.fori_loop(0, 2, first, 0)
-        kv_forward(0, 0)
-
-    ahead = jnp.where(first_section, 1, 0)
 
     def step(m, _):
-        late = m + ahead
-        new = late + 1
-
-        @pl.when(late < MICRO)
-        def _():
-            kv_forward(late, 1)
+        new = m + 1
 
         @pl.when(new < MICRO)
         def _():
             hin(new, 0)
             front(new, 0)
         with jax.named_scope("kvh"):
-            for r in range(2):
-                for i in range(2):
-                    kv_half_in(m, r, i).wait_recv()
+            kv_wait(m)
         attend(m, 0)
 
         @pl.when(new < MICRO)
@@ -530,10 +579,11 @@
         @pl.when(new < MICRO)
         def _():
             kv_forward(new, 0)
+            kv_forward(new, 1)
         project(m, 1)
         return 0
 
-    lax.fori_loop(0, MICRO, step, 0)
+    lax.fori_loop(jnp.where(first_section, 1, 0), MICRO, step, 0)
 
     with jax.named_scope("drain"):
         comm.drain()
@@ -544,9 +594,12 @@
                 def _():
                     x_send(m, r).wait_send()
                 h_fwd(m, r).wait_send()
-                for i in range(2):
-                    kv_out(m, r, i).wait_send()
-                    kv_half(m, r, i).wait_send()
+                @pl.when(m == MICRO - 1)
+                def _():
+                    for i in range(2):
+                        kv_out(m, r, i, 0).wait_send()
+                        kv_out(m, r, i, 1).wait_send()
+                        kv_half(m, r, i).wait_send()
                 a_send(m, r).wait_send()
             o_local(m).wait()
             o_sib(m).wait_send()
@@ -580,9 +633,9 @@
             pltpu.VMEM((MICRO, ROWS, 128), f32), pltpu.VMEM((MICRO, ROWS, 128), f32),
             pltpu.VMEM((MICRO, ROWS, 128), f32), pltpu.VMEM((MICRO, ROWS, 128), f32),
             pltpu.VMEM((MICRO, 1, 4 * ROWS), f32),
-            dma((N_GATHER,)), dma((N_GATHER,)),
+            dma((N_SEND,)), dma((N_GATHER,)),
             dma((MICRO, 2)), dma((MICRO, 2)), dma((MICRO, 2)), dma((MICRO, 2)),
-            dma((MICRO, 2, 4)), dma((MICRO, 2, 4)), dma((MICRO, 2)), dma((MICRO, 2)),
+            dma((2, 6)), dma((MICRO, 2, 6)), dma((MICRO, 2)), dma((MICRO, 2)),
             dma((MICRO,)), dma((MICRO,)), dma((MICRO,)),
         ],
         compiler_params=pltpu.CompilerParams(

time: 228 us -> 212 us (0.930)
  Pallas kernels: 224 us -> 208 us
    pallas_call x1, Pallas kernels: 224 us -> 208 us  [body(): pl.pallas_call(kernel, name='relay', out_shape=jax.ShapeDtypeStruct((1, M...]
where the time goes in v3:
time: 212 us
  Pallas kernels  208 us (98%)
  local copies, waits for them, and re-layouts  3.16 us (1%)
    pallas_call x1, Pallas kernels, body(): pl.pallas_call(kernel, name='relay', out_shape=jax.ShapeDtypeStruct((1, M...  208 us

profile of v3, /device:TPU:7, one launch (start us, length us, event | category | flops | bytes accessed | tf_op | source)
XLA Modules:
  0.0 212.0 jit_solution(6106668687343707582)
XLA Ops:
  0.0 0.6 maximum_bitcast_fusion.inv_ref
  0.6 208.2 %relay.1 = bf16[1,4,128,2048]{3,2,1,0:T(8,128)(2,1)} custom-call(bf16[1,32,3072]{2,1,0:T(8,128)(2,1)} %wqkv_ref.1, bf16[1,32,2048]{2,1,0:T(8,128)(2,1)} %wout_ref.1, f32[1,2048]{1,0:T(1,128)} %gain_ref.1, s32[4,8192]{1,0:T(4,128)} %pos_ref.1, s32[4,128]{1,0:T(4,128)} %doc_ref.1, f32[1,128]{1,0:T(1,128)} %maximum_bitcast_fusion.inv_ref, ...), custom_call_target="tpu_custom_call" | custom-call | tf_op jit(solution)/shard_map/relay/pallas_call | solution.py:618
  208.8 3.2 %copy.8 = bf16[1,4,128,2048]{3,2,1,0:T(8,128)(2,1)} copy(bf16[1,4,128,2048]{3,2,1,0:T(8,128)(2,1)} %relay.1) | data formatting | bytes 4194304
  (1 shorter events, 0.0 us)

commit v4 on v3

--- a/solution.py
+++ b/solution.py
@@ -569,11 +569,8 @@
         @pl.when(new < MICRO)
         def _():
             hin(new, 1)
+            front(new, 1)
         project(m, 0)
-
-        @pl.when(new < MICRO)
-        def _():
-            front(new, 1)
         attend(m, 1)
 
         @pl.when(new < MICRO)

time: 212 us -> 218 us (1.028)
  Pallas kernels: 208 us -> 214 us
    pallas_call x1, Pallas kernels: 208 us -> 214 us  [body(): pl.pallas_call(kernel, name='relay', out_shape=jax.ShapeDtypeStruct((1, M...]
where the time goes in v4:
time: 218 us
  Pallas kernels  214 us (98%)
  local copies, waits for them, and re-layouts  3.16 us (1%)
    pallas_call x1, Pallas kernels, body(): pl.pallas_call(kernel, name='relay', out_shape=jax.ShapeDtypeStruct((1, M...  214 us

profile of v4, /device:TPU:7, one launch (start us, length us, event | category | flops | bytes accessed | tf_op | source)
XLA Modules:
  0.0 217.7 jit_solution(3172141094410117443)
XLA Ops:
  0.0 0.6 maximum_bitcast_fusion.inv_ref
  0.6 213.9 %relay.1 = bf16[1,4,128,2048]{3,2,1,0:T(8,128)(2,1)} custom-call(bf16[1,32,3072]{2,1,0:T(8,128)(2,1)} %wqkv_ref.1, bf16[1,32,2048]{2,1,0:T(8,128)(2,1)} %wout_ref.1, f32[1,2048]{1,0:T(1,128)} %gain_ref.1, s32[4,8192]{1,0:T(4,128)} %pos_ref.1, s32[4,128]{1,0:T(4,128)} %doc_ref.1, f32[1,128]{1,0:T(1,128)} %maximum_bitcast_fusion.inv_ref, ...), custom_call_target="tpu_custom_call" | custom-call | tf_op jit(solution)/shard_map/relay/pallas_call | solution.py:615
  214.6 3.2 %copy.8 = bf16[1,4,128,2048]{3,2,1,0:T(8,128)(2,1)} copy(bf16[1,4,128,2048]{3,2,1,0:T(8,128)(2,1)} %relay.1) | data formatting | bytes 4194304
  (1 shorter events, 0.0 us)
